TPU v7x, 8 devices: a whole 2x2x1 slice. The times are simulated.
8 devices in a mesh: dp: 1 (over z), cols: 2 (over y), rows: 4 (over x, core).
Axes of the slice: x: 2, y: 2, z: 1, core: 2. Of those that a mesh axis runs over, the one named last changes fastest.
Arguments:
- frames: bfloat16 [32, 1, 128, 64, 64], P(None, 'dp', 'rows', 'cols')
- w_in: bfloat16 [3, 3, 64, 768], replicated
- w_rec: bfloat16 [3, 3, 192, 768], replicated
- gate_bias: float32 [768], replicated
- h_init: bfloat16 [1, 128, 64, 192], P('dp', 'rows', 'cols')
- c_init: float32 [1, 128, 64, 192], P('dp', 'rows', 'cols')
Outputs:
- output 1: bfloat16 [32, 1, 128, 64, 192], P(None, 'dp', 'rows', 'cols')
- output 2: float32 [1, 128, 64, 192], P('dp', 'rows', 'cols')
All inputs are finite; a program needn't handle non-finite values.
Results may differ from a plain program's by a relative error of at most 0.00490482.
Values are sent between devices in bfloat16 or wider.
A program may use at most 1 GiB of HBM per device.

v0:
```python
import jax
import jax.numpy as jnp
from jax import lax
from jax.sharding import PartitionSpec as P, NamedSharding

CONV_DIMS = ("NHWC", "HWIO", "NHWC")


def conv_valid(operand, kernel):
    return lax.conv_general_dilated(operand, kernel, (1, 1), "VALID", dimension_numbers=CONV_DIMS, preferred_element_type=jnp.float32)


def cell_update(gate_pre, c_prev):
    gate_i, gate_f, gate_o, gate_g = jnp.split(gate_pre, 4, axis=-1)
    c_next = jax.nn.sigmoid(gate_f) * c_prev + jax.nn.sigmoid(gate_i) * jnp.tanh(gate_g)
    h_next = (jax.nn.sigmoid(gate_o) * jnp.tanh(c_next)).astype(jnp.bfloat16)
    return h_next, c_next


def edge_exchange(tile_in, axis_name, axis_size, axis_dim, width):
    length = tile_in.shape[axis_dim]
    low_part = lax.slice_in_dim(tile_in, 0, width, axis=axis_dim)
    high_part = lax.slice_in_dim(tile_in, length - width, length, axis=axis_dim)
    if axis_size == 1:
        from_prev = jnp.zeros_like(high_part)
        from_next = jnp.zeros_like(low_part)
    else:
        forward = [(source, source + 1) for source in range(axis_size - 1)]
        backward = [(source + 1, source) for source in range(axis_size - 1)]
        from_prev = lax.ppermute(high_part, axis_name, forward)
        from_next = lax.ppermute(low_part, axis_name, backward)
    return jnp.concatenate([from_prev, tile_in, from_next], axis=axis_dim)


def add_halo(tile_in, width, n_rows, n_cols):
    row_dim = tile_in.ndim - 3
    tall_tile = edge_exchange(tile_in, "rows", n_rows, row_dim, width)
    return edge_exchange(tall_tile, "cols", n_cols, row_dim + 1, width)


def solution(mesh):
    n_rows = mesh.shape["rows"]
    n_cols = mesh.shape["cols"]
    seq_spec = P(None, "dp", "rows", "cols", None)
    state_spec = P("dp", "rows", "cols", None)

    def local_run(frames, w_in, w_rec, gate_bias, h_init, c_init):
        frames_ext = add_halo(frames, 1, n_rows, n_cols)

        def time_step(carry_in, frame_ext):
            h_prev, c_prev = carry_in
            h_ext = add_halo(h_prev, 1, n_rows, n_cols)
            gate_pre = conv_valid(frame_ext, w_in) + conv_valid(h_ext, w_rec) + gate_bias
            h_next, c_next = cell_update(gate_pre, c_prev)
            return (h_next, c_next), h_next

        (h_last, c_last), hidden_seq = lax.scan(time_step, (h_init, c_init), frames_ext)
        return hidden_seq, c_last

    return jax.shard_map(local_run, mesh=mesh, in_specs=(seq_spec, P(), P(), P(), state_spec, state_spec), out_specs=(seq_spec, state_spec), check_vma=False)
```

profile of v0, /device:TPU:1, one launch (start us, length us, event | category | flops | bytes accessed | tf_op | source)
XLA Modules:
  0.0 993.2 jit_solution(6260495492636996624)
XLA Ops:
  0.6 10.6 %copy.15 = bf16[32,1,32,32,64]{4,2,3,1,0:T(8,128)(2,1)} copy(bf16[32,1,32,32,64]{4,3,2,1,0:T(8,128)(2,1)} %param.8) | data formatting | bytes 8388608 | tf_op args[0]
  25.3 4.6 collective-permute-done.5
  43.3 14.6 %pad_maximum_fusion.3 = bf16[32,1,34,34,64]{4,2,3,1,0:T(8,128)(2,1)} fusion(bf16[32,1,34,1,64]{4,2,3,1,0:T(8,128)(2,1)} %collective-permute-done.7, bf16[32,1,1,32,64]{4,2,3,1,0:T(2,128)(2,1)S(1)} %collective-permute-done.5, bf16[32,1,32,32,64]{4,2,3,1,0:T(8,128)(2,1)} %copy.15, bf16[32,1,1,32,64]{4,2,3,1,0:T(2,128)(2,1)S(1)} %collective-permute-done.4, ...), kind=kLoop, calls=%fused_computation.51 | loop fusion | flops 23674880 | bytes 9469952 | tf_op jit(solution)/shard_map/concatenate | solution.py:32
  57.8 933.8 %while.14 = (s32[]{:T(128)}, bf16[1,32,32,192]{3,1,2,0:T(8,128)(2,1)S(1)}, f32[1,32,32,192]{3,1,2,0:T(8,128)S(1)}, bf16[32,1,32,32,192]{4,3,2,1,0:T(8,128)(2,1)}...) while((s32[]{:T(128)}, ...), condition=%wide.region_1.2_spmd, body=%wide.region_0.1_spmd.sunk | while | flops 4542246912 | bytes 53504896 | solution.py:57
  75.7 6.2 add_add_fusion.2
  88.3 4.6 collective-permute-start.1
  104.9 6.2 add_add_fusion.2
  117.5 4.5 collective-permute-start.1
  134.1 6.2 add_add_fusion.2
  146.7 4.5 collective-permute-start.1
  163.3 6.2 add_add_fusion.2
  175.9 4.5 collective-permute-start.1
  192.5 6.2 add_add_fusion.2
  205.1 4.6 collective-permute-start.1
  221.7 6.2 add_add_fusion.2
  234.3 4.5 collective-permute-start.1
  250.9 6.2 add_add_fusion.2
  263.5 4.5 collective-permute-start.1
  280.1 6.2 add_add_fusion.2
  292.7 4.5 collective-permute-start.1
  309.3 6.2 add_add_fusion.2
  321.9 4.5 collective-permute-start.1
  338.5 6.2 add_add_fusion.2
  351.1 4.6 collective-permute-start.1
  367.7 6.2 add_add_fusion.2
  380.4 4.5 collective-permute-start.1
  396.9 6.2 add_add_fusion.2
  409.6 4.5 collective-permute-start.1
  426.2 6.2 add_add_fusion.2
  438.8 4.5 collective-permute-start.1
  455.4 6.2 add_add_fusion.2
  468.0 4.5 collective-permute-start.1
  484.6 6.2 add_add_fusion.2
  497.2 4.6 collective-permute-start.1
  513.8 6.2 add_add_fusion.2
  543.0 6.2 add_add_fusion.2
  555.6 4.5 collective-permute-start.1
  572.2 6.2 add_add_fusion.2
  584.8 4.5 collective-permute-start.1
  601.4 6.2 add_add_fusion.2
  614.0 4.5 collective-permute-start.1
  630.6 6.2 add_add_fusion.2
  643.2 4.6 collective-permute-start.1
  659.8 6.2 add_add_fusion.2
  689.0 6.2 add_add_fusion.2
  701.6 4.5 collective-permute-start.1
  718.2 6.2 add_add_fusion.2
  730.8 4.5 collective-permute-start.1
  747.4 6.2 add_add_fusion.2
  760.1 4.5 collective-permute-start.1
  776.6 6.2 add_add_fusion.2
  789.3 4.6 collective-permute-start.1
  805.9 6.2 add_add_fusion.2
  818.5 4.5 collective-permute-start.1
  835.1 6.2 add_add_fusion.2
  847.7 4.5 collective-permute-start.1
  864.3 6.2 add_add_fusion.2
  876.9 4.5 collective-permute-start.1
  893.5 6.2 add_add_fusion.2
  906.1 4.5 collective-permute-start.1
  922.7 6.2 add_add_fusion.2
  935.3 4.6 collective-permute-start.1
  951.9 6.2 add_add_fusion.2
  981.1 6.2 add_add_fusion.2
  (919 shorter events, 630.6 us)
Async XLA Ops:
  14.7 10.6 %collective-permute-start.4 = (bf16[32,1,1,32,64]{4,2,3,1,0:T(2,128)(2,1)S(1)}, bf16[32,1,1,32,64]{4,2,3,1,0:T(2,128)(2,1)S(1)}, u32[]{:S(2)}, u32[]{:S(2)}) collective-permute-start(bf16[32,1,1,32,64]{4,2,3,1,0:T(2,128)(2,1)S(1)} %get-tuple-element.84), channel_id=1, source_target_pairs={{0,1},{1,2},{2,3},{4,5},{5,6},{6,7}} | collective-permute-start | bytes 393224 | tf_op jit(solution)/shard_map/ppermute | solution.py:30
  19.2 10.6 %collective-permute-start.5 = (bf16[32,1,1,32,64]{4,2,3,1,0:T(2,128)(2,1)S(1)}, bf16[32,1,1,32,64]{4,2,3,1,0:T(2,128)(2,1)S(1)}, u32[]{:S(2)}, u32[]{:S(2)}) collective-permute-start(bf16[32,1,1,32,64]{4,2,3,1,0:T(2,128)(2,1)S(1)} %get-tuple-element.85), channel_id=1, source_target_pairs={{1,0},{2,1},{3,2},{5,4},{6,5},{7,6}} | collective-permute-start | bytes 393224 | tf_op jit(solution)/shard_map/ppermute | solution.py:31
  64.9 9.0 collective-permute-start.2
  86.2 7.8 collective-permute-start
  94.1 9.0 collective-permute-start.2
  115.4 7.8 collective-permute-start
  123.3 9.0 collective-permute-start.2
  144.6 7.8 collective-permute-start
  152.5 9.0 collective-permute-start.2
  173.8 7.8 collective-permute-start
  181.7 9.0 collective-permute-start.2
  203.0 7.8 collective-permute-start
  210.9 9.0 collective-permute-start.2
  232.3 7.8 collective-permute-start
  240.1 9.0 collective-permute-start.2
  261.5 7.8 collective-permute-start
  269.3 9.0 collective-permute-start.2
  290.7 7.8 collective-permute-start
  298.6 9.0 collective-permute-start.2
  319.9 7.8 collective-permute-start
  327.8 9.0 collective-permute-start.2
  349.1 7.8 collective-permute-start
  357.0 9.0 collective-permute-start.2
  378.3 7.8 collective-permute-start
  386.2 9.0 collective-permute-start.2
  407.5 7.8 collective-permute-start
  415.4 9.0 collective-permute-start.2
  436.7 7.8 collective-permute-start
  444.6 9.0 collective-permute-start.2
  465.9 7.8 collective-permute-start
  473.8 9.0 collective-permute-start.2
  495.1 7.8 collective-permute-start
  503.0 9.0 collective-permute-start.2
  524.3 7.8 collective-permute-start
  532.2 9.0 collective-permute-start.2
  553.5 7.8 collective-permute-start
  561.4 9.0 collective-permute-start.2
  582.7 7.8 collective-permute-start
  590.6 9.0 collective-permute-start.2
  612.0 7.8 collective-permute-start
  619.8 9.0 collective-permute-start.2
  641.2 7.8 collective-permute-start
  649.0 9.0 collective-permute-start.2
  670.4 7.8 collective-permute-start
  678.2 9.0 collective-permute-start.2
  699.6 7.8 collective-permute-start
  707.5 9.0 collective-permute-start.2
  728.8 7.8 collective-permute-start
  736.7 9.0 collective-permute-start.2
  758.0 7.8 collective-permute-start
  765.9 9.0 collective-permute-start.2
  787.2 7.8 collective-permute-start
  795.1 9.0 collective-permute-start.2
  816.4 7.8 collective-permute-start
  824.3 9.0 collective-permute-start.2
  845.6 7.8 collective-permute-start
  853.5 9.0 collective-permute-start.2
  874.8 7.8 collective-permute-start
  882.7 9.0 collective-permute-start.2
  904.0 7.8 collective-permute-start
  911.9 9.0 collective-permute-start.2
  933.2 7.8 collective-permute-start
  941.1 9.0 collective-permute-start.2
  970.3 9.0 collective-permute-start.2
  (135 other events, 995.7 us)
where the time goes:
time: 1000 us; the launch traced here: 993 us
  starting transfers between devices  391 us (39%)
  matrix products  319 us (32%)
  local copies, waits for them, and re-layouts  177 us (18%)
  other arithmetic  87.5 us (9%)
  waiting for transfers between devices  13.2 us (1%)
    conv_general_dilated x64, matrix products, conv_valid(): lax.conv_general_dilated(operand, kernel, (1, 1), 'VALID', dimension_numb...  319 us
    ppermute x66, starting transfers between devices, edge_exchange(): from_prev = lax.ppermute(high_part, axis_name, forward)  281 us
    ppermute x66, starting transfers between devices, edge_exchange(): from_next = lax.ppermute(low_part, axis_name, backward)  110 us
    div x32, other arithmetic, cell_update(): jax.nn.sigmoid(gate_f) * c_prev + jax.nn.sigmoid(gate_i) * jnp.tanh(gate_g)  39.1 us
    squeeze x64, local copies, waits for them, and re-layouts, local_run(): lax.scan(time_step, (h_init, c_init), frames_ext)  35 us
    dynamic_update_slice x32, local copies, waits for them, and re-layouts, local_run(): lax.scan(time_step, (h_init, c_init), frames_ext)  34.9 us
    while x128, local copies, waits for them, and re-layouts  33.1 us
    div x64, local copies, waits for them, and re-layouts, cell_update(): jax.nn.sigmoid(gate_f) * c_prev + jax.nn.sigmoid(gate_i) * jnp.tanh(gate_g)  27.1 us
  transfers between devices with their start and end apart: 132, of which 3 were waited for; matrix products, arithmetic and copies ran while one was open for 16% of the time, Pallas kernels for 0%

commit v1 on v0

v1 whole, which is shorter than its diff:
```python
import functools

import jax
import jax.numpy as jnp
from jax import lax
from jax.experimental import pallas as pl
from jax.experimental.pallas import tpu as pltpu
from jax.sharding import PartitionSpec as P

MESH = pl.DeviceIdType.MESH
BF16, F32 = jnp.bfloat16, jnp.float32
PAD = 8
HALO_L, COL_0, COL_1, COL_30, COL_31, HALO_R = range(6)
UP, DOWN, LEFT, RIGHT = range(4)
UL, UR, DL, DR = range(4)


def half_tanh(x):
    return 0.5 * jnp.tanh(0.5 * x) + 0.5


def kernel(n_rows, n_cols, steps, th, tw,
           frames, w, bias, h_init, c_init, hs, c_out,
           s0, s1, s2, xm, xt, fx, em, et, cm, ct, colm, colt,
           ga, gb, gc, gd, gr, fr, ho, send, land, corner,
           send_sem, recv_sem, fr_sem, out_sem):
    row, col = lax.axis_index("rows"), lax.axis_index("cols")
    has = {UP: row > 0, DOWN: row < n_rows - 1, LEFT: col > 0, RIGHT: col < n_cols - 1}
    shifts = (s0, s1, s2)
    cells = th * tw

    def routes(slot):
        half = tw // 2
        edge = lambda place: land.at[slot, place]
        point = lambda place: corner.at[slot, place]
        return [
            (has[UP], -1, 0, send.at[UP], 0, edge(DOWN)),
            (has[DOWN], 1, 0, send.at[DOWN], 1, edge(UP)),
            (has[LEFT], 0, -1, send.at[LEFT], 2, edge(RIGHT)),
            (has[RIGHT], 0, 1, send.at[RIGHT], 3, edge(LEFT)),
            (has[UP] & has[LEFT], -1, -1, send.at[UP, pl.ds(0, half)], 4, point(DR)),
            (has[UP] & has[RIGHT], -1, 1, send.at[UP, pl.ds(half, half)], 5, point(DL)),
            (has[DOWN] & has[LEFT], 1, -1, send.at[DOWN, pl.ds(0, half)], 6, point(UR)),
            (has[DOWN] & has[RIGHT], 1, 1, send.at[DOWN, pl.ds(half, half)], 7, point(UL)),
        ]

    def copy_of(route, slot):
        _, d_row, d_col, src, index, dst = route
        return pltpu.make_async_remote_copy(
            src_ref=src, dst_ref=dst, send_sem=send_sem.at[index], recv_sem=recv_sem.at[slot, index],
            device_id={"rows": row + d_row, "cols": col + d_col}, device_id_type=MESH)

    def start_sends(slot):
        for route in routes(slot):
            @pl.when(route[0])
            def _():
                copy_of(route, slot).start()

    def wait_sends(slot):
        for route in routes(slot):
            @pl.when(route[0])
            def _():
                copy_of(route, slot).wait_send()

    def wait_recvs(slot):
        came = [has[DOWN], has[UP], has[RIGHT], has[LEFT], has[DOWN] & has[RIGHT], has[DOWN] & has[LEFT],
                has[UP] & has[RIGHT], has[UP] & has[LEFT]]
        for route, condition in zip(routes(slot), came):
            @pl.when(condition)
            def _():
                copy_of(route, slot).wait_recv()

    def frame_copy(t):
        return pltpu.make_async_copy(frames.at[jnp.minimum(t, steps - 1)], fr.at[lax.rem(t, 2)], fr_sem.at[lax.rem(t, 2)])

    def out_copy(t):
        return pltpu.make_async_copy(ho.at[lax.rem(t, 2)], hs.at[t], out_sem.at[lax.rem(t, 2)])

    lane = lax.broadcasted_iota(jnp.int32, (tw, 128), 1)
    low = lane < 64
    scale = jnp.where(low, 1.0, 0.5)
    shift = jnp.where(low, 0.0, 0.5)

    def cell(gates, c_main, c_tail, frame):
        pre = [gates(k) + bias[:, 128 * k:128 * (k + 1)] for k in range(6)]
        n_main = half_tanh(pre[1]) * c_main + half_tanh(pre[0]) * jnp.tanh(pre[3])
        h_main = half_tanh(pre[2]) * jnp.tanh(n_main)
        fore = half_tanh(pre[4])
        back = jnp.tanh(pre[5] * scale) * scale + shift
        n_tail = fore * c_tail + pltpu.roll(fore * back, 64, 1)
        h_tail = back * jnp.tanh(n_tail)
        return n_main, n_tail, h_main, jnp.where(low, frame, h_tail)

    def update_rows(g_ref, g_row, i):
        at = pl.ds(i * tw, tw)
        n_main, n_tail, x_main, x_tail = cell(
            lambda k: g_ref[pl.ds(g_row, tw), 128 * k:128 * (k + 1)], cm[at, :], ct[at, :], fx[at, :])
        cm[at, :] = n_main
        ct[at, :] = n_tail
        xm[pl.ds(PAD + i * tw, tw), :] = x_main
        xt[pl.ds(PAD + i * tw, tw), :] = x_tail

    def form_row(i, slot):
        for part, x in enumerate((xm, xt)):
            for dx in range(3):
                value = x[pl.ds(PAD + i * tw + dx - 1, tw), :].astype(BF16)
                shifts[dx][pl.ds((i + 1) * tw, tw), 128 * part:128 * (part + 1)] = value
        if slot is not None:
            ho[slot, pl.ds(i * tw, tw), 0:128] = xm[pl.ds(PAD + i * tw, tw), :].astype(BF16)
            tail = pltpu.roll(xt[pl.ds(PAD + i * tw, tw), :], 64, 1)
            ho[slot, pl.ds(i * tw, tw), 128:192] = tail[:, :64].astype(BF16)

    def convert_frame(t):
        for i in range(th):
            at = pl.ds(i * tw, tw)
            fx[at, 0:64] = fr[lax.rem(t, 2), at, :].astype(F32)

    def column(x, j, start=0, size=th):
        return x[pl.ds(PAD + start * tw + j, size, stride=tw), :]

    def matmul(g_ref, i, n):
        lhs = [shifts[dx][(i + dy) * tw:(i + dy + n) * tw, :] for dy in range(3) for dx in range(3)]
        g_ref[...] = jnp.dot(jnp.concatenate(lhs, axis=1), w[...], preferred_element_type=F32)

    def ring_matmul():
        lhs = []
        for dy in range(3):
            for dx in range(3):
                pieces = [shifts[dx][dy * tw:(dy + 1) * tw, :], shifts[dx][(th - 1 + dy) * tw:(th + dy) * tw, :]]
                for k in ((HALO_L, COL_0, COL_1)[dx], (COL_30, COL_31, HALO_R)[dx]):
                    at = pl.ds(PAD - 1 + dy, th)
                    pieces.append(jnp.concatenate([em[k, at, :].astype(BF16), et[k, at, :].astype(BF16)], axis=1))
                lhs.append(jnp.concatenate(pieces, axis=0))
        gr[...] = jnp.dot(jnp.concatenate(lhs, axis=1), w[...], preferred_element_type=F32)

    def place_halo(slot):
        for place, r, e_row in ((UP, 0, PAD - 1), (DOWN, th + 1, PAD + th)):
            for part, e in enumerate((em, et)):
                x = (xm, xt)[part]
                lanes = slice(128 * part, 128 * (part + 1))
                value = land[slot, place, :, lanes].astype(F32)
                s1[r * tw:(r + 1) * tw, lanes] = value.astype(BF16)
                s0[r * tw:(r + 1) * tw, lanes] = pltpu.roll(value, 1, 0).astype(BF16)
                s2[r * tw:(r + 1) * tw, lanes] = pltpu.roll(value, tw - 1, 0).astype(BF16)
                for k, j in ((COL_0, 0), (COL_1, 1), (COL_30, tw - 2), (COL_31, tw - 1)):
                    e[k, e_row:e_row + 1, :] = value[j:j + 1, :]
        for part, e in enumerate((em, et)):
            lanes = slice(128 * part, 128 * (part + 1))
            for k, place in ((HALO_L, LEFT), (HALO_R, RIGHT)):
                e[k, PAD:PAD + th, :] = land[slot, place, :, lanes].astype(F32)
            for k, e_row, place, j in ((HALO_L, PAD - 1, UL, 15), (HALO_R, PAD - 1, UR, 0),
                                       (HALO_L, PAD + th, DL, 15), (HALO_R, PAD + th, DR, 0)):
                value = corner[slot, place, :, lanes].astype(F32)
                e[k, e_row:e_row + 1, :] = value[j:j + 1, :]

    def update_ring():
        update_rows(gr, 0, 0)
        update_rows(gr, tw, th - 1)
        for index, (k, j, g_row, place) in enumerate(((COL_0, 0, 2 * tw, LEFT), (COL_31, tw - 1, 2 * tw + th, RIGHT))):
            at = pl.ds(index * th, th)
            n_main, n_tail, x_main, x_tail = cell(
                lambda p: gr[pl.ds(g_row, th), 128 * p:128 * (p + 1)], colm[at, :], colt[at, :],
                fx[pl.ds(j, th, stride=tw), :])
            colm[at, :] = n_main
            colt[at, :] = n_tail
            for part, (x, e, value) in enumerate(((xm, em, x_main), (xt, et, x_tail))):
                e[k, PAD:PAD + th, :] = value
                x[pl.ds(PAD + j, th, stride=tw), :] = value
                send[place, :, 128 * part:128 * (part + 1)] = value.astype(BF16)
        fill_row_sends()

    def fill_row_sends():
        for place, i in ((UP, 0), (DOWN, th - 1)):
            for part, x in enumerate((xm, xt)):
                send[place, :, 128 * part:128 * (part + 1)] = x[pl.ds(PAD + i * tw, tw), :].astype(BF16)

    def finish_last(slot):
        for i in range(25, 31):
            update_rows(gd, (i - 25) * tw, i)
        for k, j in ((COL_0, 0), (COL_31, tw - 1)):
            for x, e in ((xm, em), (xt, et)):
                x[pl.ds(PAD + 24 * tw + j, 8, stride=tw), :] = e[k, PAD + 24:PAD + 32, :]
        for i in range(24, 32):
            form_row(i, slot)
        for k, j in ((COL_1, 1), (COL_30, tw - 2)):
            em[k, PAD:PAD + th, :] = column(xm, j)
            et[k, PAD:PAD + th, :] = column(xt, j)

    def first_blocks():
        matmul(ga, 1, 8)
        matmul(gb, 9, 8)
        for i in range(1, 9):
            update_rows(ga, (i - 1) * tw, i)
        matmul(gc, 17, 8)
        for i in range(9, 17):
            update_rows(gb, (i - 9) * tw, i)

    def late_blocks(slot):
        ring_matmul()
        for i in range(17, 25):
            update_rows(gc, (i - 17) * tw, i)
        matmul(gd, 25, 6)
        update_ring()
        for i in range(24):
            form_row(i, slot)

    frame_copy(0).start()
    frame_copy(1).start()
    land[...] = jnp.zeros_like(land)
    corner[...] = jnp.zeros_like(corner)
    for ref in (em, et):
        ref[...] = jnp.zeros_like(ref)
    for ref in (xm, xt):
        ref[0:PAD, :] = jnp.zeros((PAD, 128), F32)
        ref[PAD + cells:, :] = jnp.zeros((PAD, 128), F32)
    fx[...] = jnp.zeros_like(fx)

    barrier = pltpu.get_barrier_semaphore()
    neighbours = 0
    for condition, d_row, d_col, *_ in routes(0):
        neighbours = neighbours + condition.astype(jnp.int32)

        @pl.when(condition)
        def _():
            pl.semaphore_signal(barrier, inc=1, device_id={"rows": row + d_row, "cols": col + d_col}, device_id_type=MESH)
    pl.semaphore_wait(barrier, neighbours)

    frame_copy(0).wait()

    @pl.loop(0, th)
    def _(i):
        at = pl.ds(pl.multiple_of(i * tw, tw), tw)
        to = pl.ds(pl.multiple_of(PAD + i * tw, 8), tw)
        fx[at, 0:64] = fr[0, at, :].astype(F32)
        xm[to, :] = h_init[at, 0:128].astype(F32)
        tail = h_init[at, 128:192].astype(F32)
        xt[to, :] = jnp.concatenate([fx[at, 0:64], tail], axis=1)
        cm[at, :] = c_init[at, 0:128]
        tail = c_init[at, 128:192]
        ct[at, :] = jnp.concatenate([tail, tail], axis=1)

    for index, (k, j, place) in enumerate(((COL_0, 0, LEFT), (COL_31, tw - 1, RIGHT))):
        at = pl.ds(index * th, th)
        colm[at, :] = cm[pl.ds(j, th, stride=tw), :]
        colt[at, :] = ct[pl.ds(j, th, stride=tw), :]
        for part, (x, e) in enumerate(((xm, em), (xt, et))):
            value = column(x, j)
            e[k, PAD:PAD + th, :] = value
            send[place, :, 128 * part:128 * (part + 1)] = value.astype(BF16)
    for k, j in ((COL_1, 1), (COL_30, tw - 2)):
        em[k, PAD:PAD + th, :] = column(xm, j)
        et[k, PAD:PAD + th, :] = column(xt, j)
    fill_row_sends()
    start_sends(0)
    frame_copy(1).wait()
    frame_copy(2).start()
    for i in range(th):
        form_row(i, None)
    convert_frame(1)
    first_blocks()

    def arrive(t):
        slot = lax.rem(t, 2)
        wait_recvs(slot)
        wait_sends(slot)
        place_halo(slot)

    def body(t, carry):
        slot = lax.rem(t, 2)
        frame_copy(t + 2).wait()
        frame_copy(t + 3).start()

        @pl.when(t >= 2)
        def _():
            out_copy(t - 2).wait()

        @pl.when(t >= 1)
        def _():
            out_copy(t - 1).start()
        arrive(t)
        late_blocks(slot)
        start_sends(1 - slot)
        finish_last(slot)
        convert_frame(t + 2)
        first_blocks()
        return carry

    lax.fori_loop(0, steps - 1, body, 0)

    last = steps - 1
    frame_copy(last + 2).wait()
    out_copy(last - 2).wait()
    out_copy(last - 1).start()
    arrive(last)
    late_blocks(last % 2)
    finish_last(last % 2)
    out_copy(last).start()
    for index, j in enumerate((0, tw - 1)):
        at = pl.ds(index * th, th)
        cm[pl.ds(j, th, stride=tw), :] = colm[at, :]
        ct[pl.ds(j, th, stride=tw), :] = colt[at, :]

    @pl.loop(0, th)
    def _(i):
        at = pl.ds(pl.multiple_of(i * tw, tw), tw)
        c_out[at, 0:128] = cm[at, :]
        c_out[at, 128:192] = pltpu.roll(ct[at, :], 64, 1)[:, :64]
    out_copy(last - 1).wait()
    out_copy(last).wait()


def lane_order(x, c):
    i, f, o, g = (x[..., k * c:(k + 1) * c] for k in range(4))
    return jnp.concatenate([i[..., :128], f[..., :128], o[..., :128], g[..., :128],
                            i[..., 128:], f[..., 128:], g[..., 128:], o[..., 128:]], axis=-1)


def solution(mesh):
    n_rows, n_cols = mesh.shape["rows"], mesh.shape["cols"]
    seq_spec = P(None, "dp", "rows", "cols", None)
    state_spec = P("dp", "rows", "cols", None)

    def local_run(frames, w_in, w_rec, gate_bias, h_init, c_init):
        steps, _, th, tw, c_in = frames.shape
        c_hid = h_init.shape[-1]
        cells = th * tw
        w = jnp.concatenate([w_rec[:, :, :128], w_in, w_rec[:, :, 128:]], axis=2)
        w = lane_order(w.reshape(9 * (c_in + c_hid), 4 * c_hid), c_hid)
        bias = lane_order(gate_bias.reshape(1, 4 * c_hid), c_hid)
        vmem = pl.BlockSpec(memory_space=pltpu.VMEM)
        hbm = pl.BlockSpec(memory_space=pl.ANY)
        run = pl.pallas_call(
            functools.partial(kernel, n_rows, n_cols, steps, th, tw),
            out_shape=(jax.ShapeDtypeStruct((steps, cells, c_hid), BF16), jax.ShapeDtypeStruct((cells, c_hid), F32)),
            in_specs=[hbm, vmem, vmem, vmem, vmem],
            out_specs=(hbm, vmem),
            scratch_shapes=[
                *[pltpu.VMEM(((th + 2) * tw, 256), BF16)] * 3,
                *[pltpu.VMEM((cells + 2 * PAD, 128), F32)] * 2,
                pltpu.VMEM((cells, 128), F32),
                *[pltpu.VMEM((6, th + 2 * PAD, 128), F32)] * 2,
                *[pltpu.VMEM((cells, 128), F32)] * 2,
                *[pltpu.VMEM((2 * th, 128), F32)] * 2,
                *[pltpu.VMEM((8 * tw, 768), F32)] * 3,
                pltpu.VMEM((6 * tw, 768), F32),
                pltpu.VMEM((4 * tw, 768), F32),
                pltpu.VMEM((2, cells, c_in), BF16),
                pltpu.VMEM((2, cells, c_hid), BF16),
                pltpu.VMEM((4, tw, 256), BF16),
                pltpu.VMEM((2, 4, tw, 256), BF16),
                pltpu.VMEM((2, 4, tw // 2, 256), BF16),
                pltpu.SemaphoreType.DMA((8,)),
                pltpu.SemaphoreType.DMA((2, 8)),
                pltpu.SemaphoreType.DMA((2,)),
                pltpu.SemaphoreType.DMA((2,)),
            ],
            compiler_params=pltpu.CompilerParams(collective_id=0, has_side_effects=True, vmem_limit_bytes=60 << 20),
        )
        hidden, c_last = run(frames.reshape(steps, cells, c_in), w, bias,
                             h_init.reshape(cells, c_hid), c_init.reshape(cells, c_hid))
        return hidden.reshape(steps, 1, th, tw, c_hid), c_last.reshape(1, th, tw, c_hid)

    return jax.shard_map(local_run, mesh=mesh, in_specs=(seq_spec, P(), P(), P(), state_spec, state_spec),
                         out_specs=(seq_spec, state_spec), check_vma=False)
```

time: 1000 us -> 190 us (0.19)
  starting transfers between devices: 391 us -> 0 us
  matrix products: 319 us -> 0 us
  Pallas kernels: 0 us -> 162 us
  local copies, waits for them, and re-layouts: 177 us -> 26.2 us
  other arithmetic: 87.5 us -> 0.42 us
  waiting for transfers between devices: 13.2 us -> 0 us
    ppermute x132 -> x0, starting transfers between devices: 391 us -> none  [the longest x66 281 us: edge_exchange(): from_prev = lax.ppermute(high_part, axis_name, forward)]
    conv_general_dilated x64 -> x0, matrix products: 319 us -> none  [conv_valid(): lax.conv_general_dilated(operand, kernel, (1, 1), 'VALID', dimension_numb...]
    pallas_call x0 -> x1, Pallas kernels: none -> 162 us  [local_run(): run(frames.reshape(steps, cells, c_in), w, bias, h_init.reshape(cells, c_...]
    div x32 -> x0, other arithmetic: 39.1 us -> none  [cell_update(): jax.nn.sigmoid(gate_f) * c_prev + jax.nn.sigmoid(gate_i) * jnp.tanh(gate_g)]
    while x130 -> x0, local copies, waits for them, and re-layouts: 35.2 us -> none
    squeeze x64 -> x0, local copies, waits for them, and re-layouts: 35 us -> none  [local_run(): lax.scan(time_step, (h_init, c_init), frames_ext)]
    dynamic_update_slice x32 -> x0, local copies, waits for them, and re-layouts: 34.9 us -> none  [local_run(): lax.scan(time_step, (h_init, c_init), frames_ext)]
    div x64 -> x0, local copies, waits for them, and re-layouts: 27.1 us -> none  [cell_update(): jax.nn.sigmoid(gate_f) * c_prev + jax.nn.sigmoid(gate_i) * jnp.tanh(gate_g)]
  transfers between devices with their start and end apart: 132 -> 0, of which waited for: 3 -> 0; matrix products, arithmetic and copies ran while one was open for 16% -> 0% of each run, Pallas kernels for 0% -> 0%
where the time goes in v1:
time: 190 us
  Pallas kernels  162 us (85%)
  local copies, waits for them, and re-layouts  26.2 us (14%)
    pallas_call x1, Pallas kernels, local_run(): run(frames.reshape(steps, cells, c_in), w, bias, h_init.reshape(cells, c_...  162 us
    unnamed x6, local copies, waits for them, and re-layouts  15 us
    concatenate x2, local copies, waits for them, and re-layouts, lane_order(): jnp.concatenate([i[..., :128], f[..., :128], o[..., :128], g[..., :128],...  7.56 us

profile of v1, /device:TPU:1, one launch (start us, length us, event | category | flops | bytes accessed | tf_op | source)
XLA Modules:
  0.0 189.8 jit_solution(16212443624160819547)
XLA Ops:
  0.6 0.0 slice-start
  0.6 0.0 slice-start.1
  0.7 0.0 copy-start.1
  0.7 0.8 reshape.27
  1.5 0.1 fusion.3
  1.6 0.6 fusion.2
  2.2 1.4 concatenate.11.bias
  3.6 0.0 slice-done
  3.6 0.0 slice-done.1
  3.6 0.0 copy-done.1
  3.6 0.4 pad_maximum_fusion
  4.0 0.6 fusion.1
  4.6 1.5 fusion
  6.1 6.2 %concatenate.10.w = bf16[2304,768]{1,0:T(8,128)(2,1)} concatenate(bf16[2304,128]{1,0:T(8,128)(2,1)S(1)} %get-tuple-element.15, bf16[2304,128]{1,0:T(8,128)(2,1)S(1)} %get-tuple-element.14, bf16[2304,128]{1,0:T(8,128)(2,1)S(1)} %get-tuple-element.13, bf16[2304,128]{1,0:T(8,128)(2,1)S(1)} %get-tuple-element.12, bf16[2304,64]{1,0:T(8,128)(2,1)} %get-tuple-element.11, ...), dimensions={1} | concatenate | bytes 7077888 | tf_op jit(solution)/shard_map/concatenate | solution.py:314
  12.3 162.5 %shard_map.77 = (bf16[32,1024,192]{2,1,0:T(8,128)(2,1)}, f32[1024,192]{1,0:T(8,128)}) custom-call(bf16[32,1024,64]{2,1,0:T(8,128)(2,1)} %bitcast.11, bf16[2304,768]{1,0:T(8,128)(2,1)} %concatenate.10.w, f32[1,768]{1,0:T(1,128)} %concatenate.11.bias, bf16[1024,192]{1,0:T(8,128)(2,1)} %bitcast.14, f32[1024,192]{1,0:T(8,128)} %bitcast.12), custom_call_target="tpu_custom_call" | custom-call | tf_op jit(solution)/shard_map/pallas_call | solution.py:359
  174.8 0.0 copy-start
  174.8 14.0 %copy.11 = bf16[32,1,32,32,192]{4,3,2,1,0:T(8,128)(2,1)} copy(bf16[32,1,32,32,192]{4,3,2,1,0:T(8,128)(2,1)} %bitcast.10) | data formatting | bytes 25165824
  188.8 0.0 copy-done
  188.8 1.0 copy.12
Async XLA Ops:
  0.6 2.9 %slice-start = ((bf16[3,3,192,768]{3,2,1,0:T(8,128)(2,1)}), bf16[3,3,64,768]{3,2,1,0:T(8,128)(2,1)S(1)}, s32[]{:S(2)}) async-start(bf16[3,3,192,768]{3,2,1,0:T(8,128)(2,1)} %param.8), calls=%async_computation | async-start | bytes 1769472 | tf_op jit(solution)/shard_map/slice | solution.py:327
  0.6 2.9 %slice-start.1 = ((bf16[3,3,192,768]{3,2,1,0:T(8,128)(2,1)}), bf16[3,3,128,768]{3,2,1,0:T(8,128)(2,1)S(1)}, s32[]{:S(2)}) async-start(bf16[3,3,192,768]{3,2,1,0:T(8,128)(2,1)} %param.8), calls=%async_computation.1 | async-start | bytes 3538944 | tf_op jit(solution)/shard_map/slice | solution.py:327
  0.7 2.9 %copy-start.1 = (bf16[3,3,64,768]{3,2,1,0:T(8,128)(2,1)S(1)}, bf16[3,3,64,768]{3,2,1,0:T(8,128)(2,1)}, u32[]{:S(2)}) copy-start(bf16[3,3,64,768]{3,2,1,0:T(8,128)(2,1)} %param.7) | copy-start | bytes 2654212
  174.8 14.0 %copy-start = (f32[1024,192]{1,0:T(8,128)S(1)}, f32[1024,192]{1,0:T(8,128)}, u32[]{:S(2)}) copy-start(f32[1024,192]{1,0:T(8,128)} %get-tuple-element.5) | copy-start | bytes 2359300

commit v2 on v1

--- a/solution.py
+++ b/solution.py
@@ -13,6 +13,7 @@
 HALO_L, COL_0, COL_1, COL_30, COL_31, HALO_R = range(6)
 UP, DOWN, LEFT, RIGHT = range(4)
 UL, UR, DL, DR = range(4)
+BLOCK_A, BLOCK_B, BLOCK_C, BLOCK_D = (1, 9), (10, 9), (19, 8), (27, 4)
 
 
 def half_tanh(x):
@@ -20,10 +21,10 @@
 
 
 def kernel(n_rows, n_cols, steps, th, tw,
-           frames, w, bias, h_init, c_init, hs, c_out,
+           frames, w_in, w_rec, gate_bias, h_hbm, c_hbm, hs, c_out,
            s0, s1, s2, xm, xt, fx, em, et, cm, ct, colm, colt,
-           ga, gb, gc, gd, gr, fr, ho, send, land, corner,
-           send_sem, recv_sem, fr_sem, out_sem):
+           ga, gb, gc, gd, gr, wraw, ws, hb, cb, fr, send, land, corner,
+           send_sem, recv_sem, fr_sem, in_sem):
     row, col = lax.axis_index("rows"), lax.axis_index("cols")
     has = {UP: row > 0, DOWN: row < n_rows - 1, LEFT: col > 0, RIGHT: col < n_cols - 1}
     shifts = (s0, s1, s2)
@@ -73,9 +74,14 @@
     def frame_copy(t):
         return pltpu.make_async_copy(frames.at[jnp.minimum(t, steps - 1)], fr.at[lax.rem(t, 2)], fr_sem.at[lax.rem(t, 2)])
 
-    def out_copy(t):
-        return pltpu.make_async_copy(ho.at[lax.rem(t, 2)], hs.at[t], out_sem.at[lax.rem(t, 2)])
-
+    weight_copies = [
+        pltpu.make_async_copy(w_rec.at[:, pl.ds(0, 128)], wraw.at[:, pl.ds(0, 128)], in_sem.at[0]),
+        pltpu.make_async_copy(w_in, wraw.at[:, pl.ds(128, 64)], in_sem.at[1]),
+        pltpu.make_async_copy(w_rec.at[:, pl.ds(128, 64)], wraw.at[:, pl.ds(192, 64)], in_sem.at[2]),
+    ]
+    state_copies = [pltpu.make_async_copy(h_hbm, hb, in_sem.at[3]), pltpu.make_async_copy(c_hbm, cb, in_sem.at[4])]
+
+    bias = lane_order(gate_bias[...], 192)
     lane = lax.broadcasted_iota(jnp.int32, (tw, 128), 1)
     low = lane < 64
     scale = jnp.where(low, 1.0, 0.5)
@@ -100,15 +106,15 @@
         xm[pl.ds(PAD + i * tw, tw), :] = x_main
         xt[pl.ds(PAD + i * tw, tw), :] = x_tail
 
-    def form_row(i, slot):
+    def form_row(i, t):
         for part, x in enumerate((xm, xt)):
             for dx in range(3):
                 value = x[pl.ds(PAD + i * tw + dx - 1, tw), :].astype(BF16)
                 shifts[dx][pl.ds((i + 1) * tw, tw), 128 * part:128 * (part + 1)] = value
-        if slot is not None:
-            ho[slot, pl.ds(i * tw, tw), 0:128] = xm[pl.ds(PAD + i * tw, tw), :].astype(BF16)
+        if t is not None:
+            hs[t, pl.ds(i * tw, tw), 0:128] = xm[pl.ds(PAD + i * tw, tw), :].astype(BF16)
             tail = pltpu.roll(xt[pl.ds(PAD + i * tw, tw), :], 64, 1)
-            ho[slot, pl.ds(i * tw, tw), 128:192] = tail[:, :64].astype(BF16)
+            hs[t, pl.ds(i * tw, tw), 128:192] = tail[:, :64].astype(BF16)
 
     def convert_frame(t):
         for i in range(th):
@@ -118,9 +124,10 @@
     def column(x, j, start=0, size=th):
         return x[pl.ds(PAD + start * tw + j, size, stride=tw), :]
 
-    def matmul(g_ref, i, n):
+    def matmul(g_ref, block):
+        i, n = block
         lhs = [shifts[dx][(i + dy) * tw:(i + dy + n) * tw, :] for dy in range(3) for dx in range(3)]
-        g_ref[...] = jnp.dot(jnp.concatenate(lhs, axis=1), w[...], preferred_element_type=F32)
+        g_ref[...] = jnp.dot(jnp.concatenate(lhs, axis=1), ws[...], preferred_element_type=F32)
 
     def ring_matmul():
         lhs = []
@@ -131,7 +138,7 @@
                     at = pl.ds(PAD - 1 + dy, th)
                     pieces.append(jnp.concatenate([em[k, at, :].astype(BF16), et[k, at, :].astype(BF16)], axis=1))
                 lhs.append(jnp.concatenate(pieces, axis=0))
-        gr[...] = jnp.dot(jnp.concatenate(lhs, axis=1), w[...], preferred_element_type=F32)
+        gr[...] = jnp.dot(jnp.concatenate(lhs, axis=1), ws[...], preferred_element_type=F32)
 
     def place_halo(slot):
         for place, r, e_row in ((UP, 0, PAD - 1), (DOWN, th + 1, PAD + th)):
@@ -174,37 +181,47 @@
             for part, x in enumerate((xm, xt)):
                 send[place, :, 128 * part:128 * (part + 1)] = x[pl.ds(PAD + i * tw, tw), :].astype(BF16)
 
-    def finish_last(slot):
-        for i in range(25, 31):
-            update_rows(gd, (i - 25) * tw, i)
+    def update_block(g_ref, block):
+        for i in range(block[0], sum(block)):
+            update_rows(g_ref, (i - block[0]) * tw, i)
+
+    def finish_last():
+        update_block(gd, BLOCK_D)
+        first = th - 8
         for k, j in ((COL_0, 0), (COL_31, tw - 1)):
             for x, e in ((xm, em), (xt, et)):
-                x[pl.ds(PAD + 24 * tw + j, 8, stride=tw), :] = e[k, PAD + 24:PAD + 32, :]
-        for i in range(24, 32):
-            form_row(i, slot)
+                x[pl.ds(PAD + first * tw + j, 8, stride=tw), :] = e[k, PAD + first:PAD + th, :]
         for k, j in ((COL_1, 1), (COL_30, tw - 2)):
             em[k, PAD:PAD + th, :] = column(xm, j)
             et[k, PAD:PAD + th, :] = column(xt, j)
 
-    def first_blocks():
-        matmul(ga, 1, 8)
-        matmul(gb, 9, 8)
-        for i in range(1, 9):
-            update_rows(ga, (i - 1) * tw, i)
-        matmul(gc, 17, 8)
-        for i in range(9, 17):
-            update_rows(gb, (i - 9) * tw, i)
-
-    def late_blocks(slot):
+    def first_blocks(t, next_frame):
+        matmul(ga, BLOCK_A)
+        for i in range(sum(BLOCK_A) + 1, sum(BLOCK_B) + 1):
+            form_row(i, t)
+        if t is not None:
+            finish_last()
+        for i in range(sum(BLOCK_B) + 1, th):
+            form_row(i, t)
+        convert_frame(next_frame)
+        matmul(gb, BLOCK_B)
+        update_block(ga, BLOCK_A)
+        matmul(gc, BLOCK_C)
+        update_block(gb, BLOCK_B)
+
+    def late_blocks(t):
         ring_matmul()
-        for i in range(17, 25):
-            update_rows(gc, (i - 17) * tw, i)
-        matmul(gd, 25, 6)
+        update_block(gc, BLOCK_C)
+        matmul(gd, BLOCK_D)
         update_ring()
-        for i in range(24):
-            form_row(i, slot)
-
+        for i in range(sum(BLOCK_A) + 1):
+            form_row(i, t)
+
+    for copy in state_copies:
+        copy.start()
     frame_copy(0).start()
+    for copy in weight_copies:
+        copy.start()
     frame_copy(1).start()
     land[...] = jnp.zeros_like(land)
     corner[...] = jnp.zeros_like(corner)
@@ -226,17 +243,19 @@
     pl.semaphore_wait(barrier, neighbours)
 
     frame_copy(0).wait()
+    for copy in state_copies:
+        copy.wait()
 
     @pl.loop(0, th)
     def _(i):
         at = pl.ds(pl.multiple_of(i * tw, tw), tw)
         to = pl.ds(pl.multiple_of(PAD + i * tw, 8), tw)
         fx[at, 0:64] = fr[0, at, :].astype(F32)
-        xm[to, :] = h_init[at, 0:128].astype(F32)
-        tail = h_init[at, 128:192].astype(F32)
+        xm[to, :] = hb[at, 0:128].astype(F32)
+        tail = hb[at, 128:192].astype(F32)
         xt[to, :] = jnp.concatenate([fx[at, 0:64], tail], axis=1)
-        cm[at, :] = c_init[at, 0:128]
-        tail = c_init[at, 128:192]
+        cm[at, :] = cb[at, 0:128]
+        tail = cb[at, 128:192]
         ct[at, :] = jnp.concatenate([tail, tail], axis=1)
 
     for index, (k, j, place) in enumerate(((COL_0, 0, LEFT), (COL_31, tw - 1, RIGHT))):
@@ -254,10 +273,17 @@
     start_sends(0)
     frame_copy(1).wait()
     frame_copy(2).start()
-    for i in range(th):
+    for i in range(sum(BLOCK_A) + 1):
         form_row(i, None)
-    convert_frame(1)
-    first_blocks()
+    for copy in weight_copies:
+        copy.wait()
+
+    @pl.loop(0, 9)
+    def _(tap):
+        for k in range(0, 256, 64):
+            at = pl.ds(pl.multiple_of(tap * 256 + k, 64), 64)
+            ws[at, :] = lane_order(wraw[tap, k:k + 64, :], 192)
+    first_blocks(None, 1)
 
     def arrive(t):
         slot = lax.rem(t, 2)
@@ -269,32 +295,21 @@
         slot = lax.rem(t, 2)
         frame_copy(t + 2).wait()
         frame_copy(t + 3).start()
-
-        @pl.when(t >= 2)
-        def _():
-            out_copy(t - 2).wait()
-
-        @pl.when(t >= 1)
-        def _():
-            out_copy(t - 1).start()
         arrive(t)
-        late_blocks(slot)
+        late_blocks(t)
         start_sends(1 - slot)
-        finish_last(slot)
-        convert_frame(t + 2)
-        first_blocks()
+        first_blocks(t, t + 2)
         return carry
 
     lax.fori_loop(0, steps - 1, body, 0)
 
     last = steps - 1
     frame_copy(last + 2).wait()
-    out_copy(last - 2).wait()
-    out_copy(last - 1).start()
     arrive(last)
-    late_blocks(last % 2)
-    finish_last(last % 2)
-    out_copy(last).start()
+    late_blocks(last)
+    finish_last()
+    for i in range(sum(BLOCK_A) + 1, th):
+        form_row(i, last)
     for index, j in enumerate((0, tw - 1)):
         at = pl.ds(index * th, th)
         cm[pl.ds(j, th, stride=tw), :] = colm[at, :]
@@ -305,8 +320,6 @@
         at = pl.ds(pl.multiple_of(i * tw, tw), tw)
         c_out[at, 0:128] = cm[at, :]
         c_out[at, 128:192] = pltpu.roll(ct[at, :], 64, 1)[:, :64]
-    out_copy(last - 1).wait()
-    out_copy(last).wait()
 
 
 def lane_order(x, c):
@@ -324,16 +337,13 @@
         steps, _, th, tw, c_in = frames.shape
         c_hid = h_init.shape[-1]
         cells = th * tw
-        w = jnp.concatenate([w_rec[:, :, :128], w_in, w_rec[:, :, 128:]], axis=2)
-        w = lane_order(w.reshape(9 * (c_in + c_hid), 4 * c_hid), c_hid)
-        bias = lane_order(gate_bias.reshape(1, 4 * c_hid), c_hid)
         vmem = pl.BlockSpec(memory_space=pltpu.VMEM)
         hbm = pl.BlockSpec(memory_space=pl.ANY)
         run = pl.pallas_call(
             functools.partial(kernel, n_rows, n_cols, steps, th, tw),
-            out_shape=(jax.ShapeDtypeStruct((steps, cells, c_hid), BF16), jax.ShapeDtypeStruct((cells, c_hid), F32)),
-            in_specs=[hbm, vmem, vmem, vmem, vmem],
-            out_specs=(hbm, vmem),
+            out_shape=(pltpu.VMEM((steps, cells, c_hid), BF16), jax.ShapeDtypeStruct((cells, c_hid), F32)),
+            in_specs=[hbm, hbm, hbm, vmem, hbm, hbm],
+            out_specs=(vmem, vmem),
             scratch_shapes=[
                 *[pltpu.VMEM(((th + 2) * tw, 256), BF16)] * 3,
                 *[pltpu.VMEM((cells + 2 * PAD, 128), F32)] * 2,
@@ -341,23 +351,25 @@
                 *[pltpu.VMEM((6, th + 2 * PAD, 128), F32)] * 2,
                 *[pltpu.VMEM((cells, 128), F32)] * 2,
                 *[pltpu.VMEM((2 * th, 128), F32)] * 2,
-                *[pltpu.VMEM((8 * tw, 768), F32)] * 3,
-                pltpu.VMEM((6 * tw, 768), F32),
+                *[pltpu.VMEM((block[1] * tw, 768), F32) for block in (BLOCK_A, BLOCK_B, BLOCK_C, BLOCK_D)],
                 pltpu.VMEM((4 * tw, 768), F32),
+                pltpu.VMEM((9, c_in + c_hid, 4 * c_hid), BF16),
+                pltpu.VMEM((9 * (c_in + c_hid), 4 * c_hid), BF16),
+                pltpu.VMEM((cells, c_hid), BF16),
+                pltpu.VMEM((cells, c_hid), F32),
                 pltpu.VMEM((2, cells, c_in), BF16),
-                pltpu.VMEM((2, cells, c_hid), BF16),
                 pltpu.VMEM((4, tw, 256), BF16),
                 pltpu.VMEM((2, 4, tw, 256), BF16),
                 pltpu.VMEM((2, 4, tw // 2, 256), BF16),
                 pltpu.SemaphoreType.DMA((8,)),
                 pltpu.SemaphoreType.DMA((2, 8)),
                 pltpu.SemaphoreType.DMA((2,)),
-                pltpu.SemaphoreType.DMA((2,)),
+                pltpu.SemaphoreType.DMA((5,)),
             ],
-            compiler_params=pltpu.CompilerParams(collective_id=0, has_side_effects=True, vmem_limit_bytes=60 << 20),
+            compiler_params=pltpu.CompilerParams(collective_id=0, has_side_effects=True, vmem_limit_bytes=40 << 20),
         )
-        hidden, c_last = run(frames.reshape(steps, cells, c_in), w, bias,
-                             h_init.reshape(cells, c_hid), c_init.reshape(cells, c_hid))
+        hidden, c_last = run(frames.reshape(steps, cells, c_in), w_in.reshape(9, c_in, -1), w_rec.reshape(9, c_hid, -1),
+                             gate_bias.reshape(1, -1), h_init.reshape(cells, c_hid), c_init.reshape(cells, c_hid))
         return hidden.reshape(steps, 1, th, tw, c_hid), c_last.reshape(1, th, tw, c_hid)
 
     return jax.shard_map(local_run, mesh=mesh, in_specs=(seq_spec, P(), P(), P(), state_spec, state_spec),

time: 190 us -> 168 us (0.88)
  local copies, waits for them, and re-layouts: 26.2 us -> 8.41 us
  Pallas kernels: 162 us -> 158 us
    unnamed x6 -> x4, local copies, waits for them, and re-layouts: 15 us -> 7.14 us
    concatenate x2 -> x0, local copies, waits for them, and re-layouts: 7.56 us -> none  [lane_order(): jnp.concatenate([i[..., :128], f[..., :128], o[..., :128], g[..., :128],...]
    pallas_call x1, Pallas kernels: 162 us -> 158 us  [local_run(): run(frames.reshape(steps, cells, c_in), w_in.reshape(9, c_in, -1), w_rec....]
    slice x8 -> x0, local copies, waits for them, and re-layouts: 2.82 us -> none  [the longest x2 2.16 us: lane_order(): o[..., 128:]]
where the time goes in v2:
time: 168 us; the launch traced here: 167 us
  Pallas kernels  158 us (94%)
  local copies, waits for them, and re-layouts  8.41 us (5%)
    pallas_call x1, Pallas kernels, local_run(): run(frames.reshape(steps, cells, c_in), w_in.reshape(9, c_in, -1), w_rec....  158 us
    unnamed x4, local copies, waits for them, and re-layouts  7.14 us

profile of v2, /device:TPU:1, one launch (start us, length us, event | category | flops | bytes accessed | tf_op | source)
XLA Modules:
  0.0 167.4 jit_solution(4884579712774938291)
XLA Ops:
  0.6 1.3 reshape.31.gate_bias
  1.9 158.4 %shard_map.77 = (bf16[32,1024,192]{2,1,0:T(8,128)(2,1)S(1)}, f32[1024,192]{1,0:T(8,128)}) custom-call(bf16[32,1024,64]{2,1,0:T(8,128)(2,1)} %bitcast.10, bf16[9,64,768]{2,1,0:T(8,128)(2,1)} %bitcast.14, bf16[9,192,768]{2,1,0:T(8,128)(2,1)} %bitcast.11, f32[1,768]{1,0:T(1,128)} %reshape.31.gate_bias, bf16[1024,192]{1,0:T(8,128)(2,1)} %bitcast.15, ...), custom_call_target="tpu_custom_call" | custom-call | tf_op jit(solution)/shard_map/pallas_call | solution.py:371
  160.3 0.0 copy-start
  160.3 6.2 %copy.11 = bf16[32,1,32,32,192]{4,3,2,1,0:T(8,128)(2,1)} copy(bf16[32,1,32,32,192]{4,3,2,1,0:T(8,128)(2,1)S(1)} %bitcast.9) | data formatting | bytes 25165824
  166.5 0.0 copy-done
  166.5 1.0 copy.12
Async XLA Ops:
  160.3 6.2 %copy-start = (f32[1024,192]{1,0:T(8,128)S(1)}, f32[1024,192]{1,0:T(8,128)}, u32[]{:S(2)}) copy-start(f32[1024,192]{1,0:T(8,128)} %get-tuple-element.5) | copy-start | bytes 2359300

commit v3 on v2

v3 whole, which is shorter than its diff:
```python
import functools

import jax
import jax.numpy as jnp
from jax import lax
from jax.experimental import pallas as pl
from jax.experimental.pallas import tpu as pltpu
from jax.sharding import PartitionSpec as P

MESH = pl.DeviceIdType.MESH
BF16, F32 = jnp.bfloat16, jnp.float32
PAD = 8
PITCH = 40
UP, DOWN, LEFT, RIGHT = range(4)
UL, UR, DL, DR = range(4)
BLOCK_A, BLOCK_B, BLOCK_C, BLOCK_D = (1, 8), (9, 9), (18, 8), (26, 4)
RING_ROWS = (0, 30, 31)


def half_tanh(x):
    return 0.5 * jnp.tanh(0.5 * x) + 0.5


def kernel(n_rows, n_cols, steps, th, tw,
           frames, w_in, w_rec, gate_bias, h_hbm, c_hbm, hs, c_out,
           xm, xt, fx, em, et, cm, ct, colm, colt, ga, gb, gc, gd, gr,
           wraw, ws, hb, cb, fr, send, land, corner, send_sem, recv_sem, fr_sem, in_sem):
    row, col = lax.axis_index("rows"), lax.axis_index("cols")
    has = {UP: row > 0, DOWN: row < n_rows - 1, LEFT: col > 0, RIGHT: col < n_cols - 1}
    cells = th * tw

    def routes(slot):
        half = tw // 2
        edge = lambda place: land.at[slot, place]
        point = lambda place: corner.at[slot, place]
        return [
            (has[UP], -1, 0, send.at[UP], 0, edge(DOWN)),
            (has[DOWN], 1, 0, send.at[DOWN], 1, edge(UP)),
            (has[LEFT], 0, -1, send.at[2], 2, edge(RIGHT)),
            (has[RIGHT], 0, 1, send.at[2], 3, edge(LEFT)),
            (has[UP] & has[LEFT], -1, -1, send.at[UP, pl.ds(0, half)], 4, point(DR)),
            (has[UP] & has[RIGHT], -1, 1, send.at[UP, pl.ds(half, half)], 5, point(DL)),
            (has[DOWN] & has[LEFT], 1, -1, send.at[DOWN, pl.ds(0, half)], 6, point(UR)),
            (has[DOWN] & has[RIGHT], 1, 1, send.at[DOWN, pl.ds(half, half)], 7, point(UL)),
        ]

    def copy_of(route, slot):
        _, d_row, d_col, src, index, dst = route
        return pltpu.make_async_remote_copy(
            src_ref=src, dst_ref=dst, send_sem=send_sem.at[index], recv_sem=recv_sem.at[slot, index],
            device_id={"rows": row + d_row, "cols": col + d_col}, device_id_type=MESH)

    def start_sends(slot):
        for route in routes(slot):
            @pl.when(route[0])
            def _():
                copy_of(route, slot).start()

    def wait_sends(slot):
        for route in routes(slot):
            @pl.when(route[0])
            def _():
                copy_of(route, slot).wait_send()

    def wait_recvs(slot):
        came = [has[DOWN], has[UP], has[RIGHT], has[LEFT], has[DOWN] & has[RIGHT], has[DOWN] & has[LEFT],
                has[UP] & has[RIGHT], has[UP] & has[LEFT]]
        for route, condition in zip(routes(slot), came):
            @pl.when(condition)
            def _():
                copy_of(route, slot).wait_recv()

    def frame_copy(t, slot):
        return pltpu.make_async_copy(frames.at[jnp.minimum(t, steps - 1)], fr.at[slot], fr_sem.at[slot])

    weight_copies = [
        pltpu.make_async_copy(w_rec.at[:, pl.ds(0, 128)], wraw.at[:, pl.ds(0, 128)], in_sem.at[0]),
        pltpu.make_async_copy(w_in, wraw.at[:, pl.ds(128, 64)], in_sem.at[1]),
        pltpu.make_async_copy(w_rec.at[:, pl.ds(128, 64)], wraw.at[:, pl.ds(192, 64)], in_sem.at[2]),
    ]
    state_copies = [pltpu.make_async_copy(h_hbm, hb, in_sem.at[3]), pltpu.make_async_copy(c_hbm, cb, in_sem.at[4])]

    bias = lane_order(gate_bias[...].reshape(1, 768), 192)
    lane = lax.broadcasted_iota(jnp.int32, (tw, 128), 1)
    low = lane < 64
    scale = jnp.where(low, 1.0, 0.5)
    shift = jnp.where(low, 0.0, 0.5)
    x = (xm, xt)
    inner = (1 - col) * (tw - 1)
    edges = (em, et)
    own, beside, beyond = 1, 2 * col, 2 - 2 * col

    def base(i):
        return PAD + (i + 1) * PITCH + 8

    def row_at(i):
        return pl.ds(base(i), tw)

    def col_at(j, first=0, size=th):
        return pl.ds(base(first) + j, size, stride=PITCH)

    def dot(lhs):
        return lax.dot_general(jnp.concatenate(lhs, axis=1), ws[...], (((1,), (0,)), ((), ())), preferred_element_type=F32)

    def row_parts(rows, dy, dx):
        return [jnp.concatenate([part[pl.ds(base(i + dy - 1) + dx - 1, tw), :] for i in rows], axis=0) for part in x]

    def matmul(g_ref, block):
        rows = range(block[0], sum(block))
        g_ref[...] = dot([v for dy in range(3) for dx in range(3) for v in row_parts(rows, dy, dx)])

    def ring_matmul():
        lhs = []
        for dy in range(3):
            for dx in range(3):
                for part, value in enumerate(row_parts(RING_ROWS, dy, dx)):
                    lhs.append(jnp.concatenate([value, edges[part][dx, pl.ds(PAD - 1 + dy, th), :]], axis=0))
        gr[...] = dot(lhs)

    def cell(gates, c_main, c_tail, frame):
        pre = [gates(k) + bias[:, 128 * k:128 * (k + 1)] for k in range(6)]
        n_main = half_tanh(pre[1]) * c_main + half_tanh(pre[0]) * jnp.tanh(pre[3])
        h_main = half_tanh(pre[2]) * jnp.tanh(n_main)
        fore = half_tanh(pre[4])
        back = jnp.tanh(pre[5] * scale) * scale + shift
        n_tail = fore * c_tail + pltpu.roll(fore * back, 64, 1)
        return n_main, n_tail, h_main, jnp.where(low, frame, back * jnp.tanh(n_tail))

    def update_row(g_ref, g_row, i):
        at = pl.ds(i * tw, tw)
        cm[at, :], ct[at, :], xm[row_at(i), :], xt[row_at(i), :] = cell(
            lambda k: g_ref[pl.ds(g_row, tw), 128 * k:128 * (k + 1)], cm[at, :], ct[at, :], fx[at, :])

    def update_rows(g_ref, block, rows):
        for i in rows:
            update_row(g_ref, (i - block[0]) * tw, i)

    def update_ring():
        update_row(gr, 0, 0)
        update_row(gr, 2 * tw, th - 1)
        g_row = len(RING_ROWS) * tw
        colm[...], colt[...], *values = cell(
            lambda k: gr[pl.ds(g_row, th), 128 * k:128 * (k + 1)], colm[...], colt[...], fx[pl.ds(inner, th, stride=tw), :])
        for part, value in enumerate(values):
            edges[part][own, PAD:PAD + th, :] = value
            x[part][col_at(inner, 0, th - 8), :] = value[:th - 8]
            x[part][pl.ds(base(th - 1) + inner, 1), :] = value[th - 1:]
            send[2, :, 128 * part:128 * (part + 1)] = value.astype(BF16)
        fill_row_sends()

    def fill_row_sends():
        for place, i in ((UP, 0), (DOWN, th - 1)):
            for part in range(2):
                send[place, :, 128 * part:128 * (part + 1)] = x[part][row_at(i), :].astype(BF16)

    def keep_beside():
        for part, e in enumerate(edges):
            e[beside, PAD:PAD + th, :] = x[part][col_at(inner + 1 - beyond), :]

    def finish_step():
        update_rows(gc, BLOCK_C, [25])
        update_rows(gd, BLOCK_D, range(26, 30))
        update_row(gr, tw, 30)
        for part, e in enumerate(edges):
            x[part][col_at(inner, th - 8, 8), :] = e[own, PAD + th - 8:PAD + th, :]
        keep_beside()

    def form_out(t):
        for i in range(th):
            at = pl.ds(i * tw, tw)
            hs[t, at, 0:128] = x[0][row_at(i), :].astype(BF16)
            hs[t, at, 128:192] = pltpu.roll(x[1][row_at(i), :], 64, 1)[:, :64].astype(BF16)

    def convert_frame(slot):
        for i in range(th):
            at = pl.ds(i * tw, tw)
            fx[at, 0:64] = fr[slot, at, :].astype(F32)

    def place_halo(slot):
        for part, e in enumerate(edges):
            lanes = slice(128 * part, 128 * (part + 1))
            for place, i in ((UP, -1), (DOWN, th)):
                x[part][row_at(i), :] = land[slot, place, :, lanes].astype(F32)
            for place, i, j, r in ((UL, -1, -1, 15), (UR, -1, tw, 0), (DL, th, -1, 15), (DR, th, tw, 0)):
                x[part][pl.ds(base(i) + j, 1), :] = corner[slot, place, :, lanes].astype(F32)[r:r + 1, :]
            e[beyond, PAD:PAD + th, :] = land[slot, RIGHT - col, :, lanes].astype(F32)
            for k in range(3):
                for i in (-1, th):
                    e[k, PAD + i:PAD + i + 1, :] = x[part][pl.ds(base(i) + inner - 1 + k, 1), :]

    def late_blocks():
        ring_matmul()
        update_rows(ga, BLOCK_A, [1])
        update_rows(gb, BLOCK_B, [17])
        update_rows(gc, BLOCK_C, range(18, 25))
        matmul(gd, BLOCK_D)
        update_ring()

    def early_blocks(t, frame_slot):
        matmul(ga, BLOCK_A)
        if t is not None:
            finish_step()
            form_out(t)
        convert_frame(frame_slot)
        matmul(gb, BLOCK_B)
        update_rows(ga, BLOCK_A, range(2, 8))
        matmul(gc, BLOCK_C)
        update_rows(ga, BLOCK_A, [8])
        update_rows(gb, BLOCK_B, range(9, 17))

    for copy in state_copies:
        copy.start()
    frame_copy(0, 0).start()
    for copy in weight_copies:
        copy.start()
    frame_copy(1, 1).start()
    land[...] = jnp.zeros_like(land)
    corner[...] = jnp.zeros_like(corner)
    for ref in (em, et, xm, xt):
        ref[...] = jnp.zeros_like(ref)
    fx[...] = jnp.zeros_like(fx)

    barrier = pltpu.get_barrier_semaphore()
    neighbours = 0
    for condition, d_row, d_col, *_ in routes(0):
        neighbours = neighbours + condition.astype(jnp.int32)

        @pl.when(condition)
        def _():
            pl.semaphore_signal(barrier, inc=1, device_id={"rows": row + d_row, "cols": col + d_col}, device_id_type=MESH)
    pl.semaphore_wait(barrier, neighbours)

    frame_copy(0, 0).wait()
    for copy in state_copies:
        copy.wait()

    @pl.loop(0, th)
    def _(i):
        at = pl.ds(pl.multiple_of(i * tw, tw), tw)
        to = pl.ds(pl.multiple_of(base(0) + i * PITCH, 8), tw)
        xm[to, :] = hb[at, 0:128].astype(F32)
        tail = hb[at, 128:192].astype(F32)
        xt[to, :] = jnp.concatenate([fr[0, at, :].astype(F32), tail], axis=1)
        cm[at, :] = cb[at, 0:128]
        tail = cb[at, 128:192]
        ct[at, :] = jnp.concatenate([tail, tail], axis=1)

    colm[...] = cm[pl.ds(inner, th, stride=tw), :]
    colt[...] = ct[pl.ds(inner, th, stride=tw), :]
    for part in range(2):
        value = x[part][col_at(inner), :]
        edges[part][own, PAD:PAD + th, :] = value
        send[2, :, 128 * part:128 * (part + 1)] = value.astype(BF16)
    keep_beside()
    fill_row_sends()
    start_sends(0)
    frame_copy(1, 1).wait()
    frame_copy(2, 0).start()
    for copy in weight_copies:
        copy.wait()

    @pl.loop(0, 9)
    def _(tap):
        for k in range(0, 256, 64):
            at = pl.ds(pl.multiple_of(tap * 256 + k, 64), 64)
            ws[at, :] = lane_order(wraw[tap, k:k + 64, :], 192)
    early_blocks(None, 1)

    def arrive(slot):
        wait_recvs(slot)
        wait_sends(slot)
        place_halo(slot)

    def body(t, carry):
        slot = lax.rem(t, 2)
        frame_copy(t + 2, slot).wait()
        frame_copy(t + 3, 1 - slot).start()
        arrive(slot)
        late_blocks()
        start_sends(1 - slot)
        early_blocks(t, slot)
        return carry

    last = steps - 1
    lax.fori_loop(0, last, body, 0)
    frame_copy(last + 2, last % 2).wait()
    arrive(last % 2)
    late_blocks()
    finish_step()
    form_out(last)
    cm[pl.ds(inner, th, stride=tw), :] = colm[...]
    ct[pl.ds(inner, th, stride=tw), :] = colt[...]

    @pl.loop(0, th)
    def _(i):
        at = pl.ds(pl.multiple_of(i * tw, tw), tw)
        c_out[at, 0:128] = cm[at, :]
        c_out[at, 128:192] = pltpu.roll(ct[at, :], 64, 1)[:, :64]


def lane_order(x, c):
    i, f, o, g = (x[..., k * c:(k + 1) * c] for k in range(4))
    return jnp.concatenate([i[..., :128], f[..., :128], o[..., :128], g[..., :128],
                            i[..., 128:], f[..., 128:], g[..., 128:], o[..., 128:]], axis=-1)


def solution(mesh):
    n_rows, n_cols = mesh.shape["rows"], mesh.shape["cols"]
    seq_spec = P(None, "dp", "rows", "cols", None)
    state_spec = P("dp", "rows", "cols", None)

    def local_run(frames, w_in, w_rec, gate_bias, h_init, c_init):
        steps, _, th, tw, c_in = frames.shape
        c_hid = h_init.shape[-1]
        cells = th * tw
        vmem = pl.BlockSpec(memory_space=pltpu.VMEM)
        hbm = pl.BlockSpec(memory_space=pl.ANY)
        run = pl.pallas_call(
            functools.partial(kernel, n_rows, n_cols, steps, th, tw),
            out_shape=(pltpu.VMEM((steps, cells, c_hid), BF16), pltpu.VMEM((cells, c_hid), F32)),
            in_specs=[hbm, hbm, hbm, vmem, hbm, hbm],
            out_specs=(vmem, vmem),
            scratch_shapes=[
                *[pltpu.VMEM((PAD + (th + 2) * PITCH + PAD, 128), F32)] * 2,
                pltpu.VMEM((cells, 128), F32),
                *[pltpu.VMEM((3, th + 2 * PAD, 128), F32)] * 2,
                *[pltpu.VMEM((cells, 128), F32)] * 2,
                *[pltpu.VMEM((th, 128), F32)] * 2,
                *[pltpu.VMEM((block[1] * tw, 768), F32) for block in (BLOCK_A, BLOCK_B, BLOCK_C, BLOCK_D)],
                pltpu.VMEM(((len(RING_ROWS) + 1) * tw, 768), F32),
                pltpu.VMEM((9, c_in + c_hid, 4 * c_hid), BF16),
                pltpu.VMEM((9 * (c_in + c_hid), 4 * c_hid), BF16),
                pltpu.VMEM((cells, c_hid), BF16),
                pltpu.VMEM((cells, c_hid), F32),
                pltpu.VMEM((2, cells, c_in), BF16),
                pltpu.VMEM((4, tw, 256), BF16),
                pltpu.VMEM((2, 4, tw, 256), BF16),
                pltpu.VMEM((2, 4, tw // 2, 256), BF16),
                pltpu.SemaphoreType.DMA((8,)),
                pltpu.SemaphoreType.DMA((2, 8)),
                pltpu.SemaphoreType.DMA((2,)),
                pltpu.SemaphoreType.DMA((5,)),
            ],
            compiler_params=pltpu.CompilerParams(collective_id=0, has_side_effects=True, vmem_limit_bytes=40 << 20),
        )
        hidden, c_last = run(frames.reshape(steps, cells, c_in), w_in.reshape(9, c_in, -1), w_rec.reshape(9, c_hid, -1),
                             gate_bias, h_init.reshape(cells, c_hid), c_init.reshape(cells, c_hid))
        return hidden.reshape(steps, 1, th, tw, c_hid), c_last.reshape(1, th, tw, c_hid)

    return jax.shard_map(local_run, mesh=mesh, in_specs=(seq_spec, P(), P(), P(), state_spec, state_spec),
                         out_specs=(seq_spec, state_spec), check_vma=False)
```

time: 168 us -> 155 us (0.923)
  Pallas kernels: 158 us -> 147 us
    pallas_call x1, Pallas kernels: 158 us -> 147 us  [local_run(): run(frames.reshape(steps, cells, c_in), w_in.reshape(9, c_in, -1), w_rec....]
    unnamed x4 -> x2, local copies, waits for them, and re-layouts: 7.14 us -> 7.13 us
where the time goes in v3:
time: 155 us
  Pallas kernels  147 us (95%)
  local copies, waits for them, and re-layouts  7.13 us (5%)
    pallas_call x1, Pallas kernels, local_run(): run(frames.reshape(steps, cells, c_in), w_in.reshape(9, c_in, -1), w_rec....  147 us
    unnamed x2, local copies, waits for them, and re-layouts  7.13 us

profile of v3, /device:TPU:1, one launch (start us, length us, event | category | flops | bytes accessed | tf_op | source)
XLA Modules:
  0.0 154.5 jit_solution(14347297154092857618)
XLA Ops:
  0.6 146.8 %shard_map.77 = (bf16[32,1024,192]{2,1,0:T(8,128)(2,1)S(1)}, f32[1024,192]{1,0:T(8,128)S(1)}) custom-call(bf16[32,1024,64]{2,1,0:T(8,128)(2,1)} %bitcast.11, bf16[9,64,768]{2,1,0:T(8,128)(2,1)} %bitcast.14, bf16[9,192,768]{2,1,0:T(8,128)(2,1)} %bitcast.12, f32[768]{0:T(1024)} %gate_bias.1, bf16[1024,192]{1,0:T(8,128)(2,1)} %bitcast.15, f32[1024,192]{1,0:T(8,128)} %bitcast.13), custom_call_target="tpu_custom_call" | custom-call | tf_op jit(solution)/shard_map/pallas_call | solution.py:346
  147.4 6.2 %copy.11 = bf16[32,1,32,32,192]{4,3,2,1,0:T(8,128)(2,1)} copy(bf16[32,1,32,32,192]{4,3,2,1,0:T(8,128)(2,1)S(1)} %bitcast.9) | data formatting | bytes 25165824
  153.6 1.0 copy.12

commit v4 on v3

--- a/solution.py
+++ b/solution.py
@@ -11,8 +11,7 @@
 BF16, F32 = jnp.bfloat16, jnp.float32
 PAD = 8
 PITCH = 40
-UP, DOWN, LEFT, RIGHT = range(4)
-UL, UR, DL, DR = range(4)
+UP, DOWN, SIDE = range(3)
 BLOCK_A, BLOCK_B, BLOCK_C, BLOCK_D = (1, 8), (9, 9), (18, 8), (26, 4)
 RING_ROWS = (0, 30, 31)
 
@@ -26,49 +25,41 @@
            xm, xt, fx, em, et, cm, ct, colm, colt, ga, gb, gc, gd, gr,
            wraw, ws, hb, cb, fr, send, land, corner, send_sem, recv_sem, fr_sem, in_sem):
     row, col = lax.axis_index("rows"), lax.axis_index("cols")
-    has = {UP: row > 0, DOWN: row < n_rows - 1, LEFT: col > 0, RIGHT: col < n_cols - 1}
+    above, below = row > 0, row < n_rows - 1
     cells = th * tw
+    half = tw // 2
+    near = pl.ds(pl.multiple_of((1 - col) * half, half), half)
 
     def routes(slot):
-        half = tw // 2
-        edge = lambda place: land.at[slot, place]
-        point = lambda place: corner.at[slot, place]
+        across = 1 - 2 * col
         return [
-            (has[UP], -1, 0, send.at[UP], 0, edge(DOWN)),
-            (has[DOWN], 1, 0, send.at[DOWN], 1, edge(UP)),
-            (has[LEFT], 0, -1, send.at[2], 2, edge(RIGHT)),
-            (has[RIGHT], 0, 1, send.at[2], 3, edge(LEFT)),
-            (has[UP] & has[LEFT], -1, -1, send.at[UP, pl.ds(0, half)], 4, point(DR)),
-            (has[UP] & has[RIGHT], -1, 1, send.at[UP, pl.ds(half, half)], 5, point(DL)),
-            (has[DOWN] & has[LEFT], 1, -1, send.at[DOWN, pl.ds(0, half)], 6, point(UR)),
-            (has[DOWN] & has[RIGHT], 1, 1, send.at[DOWN, pl.ds(half, half)], 7, point(UL)),
+            (above, -1, 0, send.at[UP], land.at[slot, DOWN]),
+            (below, 1, 0, send.at[DOWN], land.at[slot, UP]),
+            (None, 0, across, send.at[SIDE], land.at[slot, SIDE]),
+            (above, -1, across, send.at[UP, near], corner.at[slot, DOWN]),
+            (below, 1, across, send.at[DOWN, near], corner.at[slot, UP]),
         ]
 
-    def copy_of(route, slot):
-        _, d_row, d_col, src, index, dst = route
-        return pltpu.make_async_remote_copy(
-            src_ref=src, dst_ref=dst, send_sem=send_sem.at[index], recv_sem=recv_sem.at[slot, index],
-            device_id={"rows": row + d_row, "cols": col + d_col}, device_id_type=MESH)
+    def guarded(condition, run):
+        run() if condition is None else pl.when(condition)(run)
+
+    def copies(slot):
+        for index, (condition, d_row, d_col, src, dst) in enumerate(routes(slot)):
+            yield condition, pltpu.make_async_remote_copy(
+                src_ref=src, dst_ref=dst, send_sem=send_sem.at[index], recv_sem=recv_sem.at[slot, index],
+                device_id={"rows": row + d_row, "cols": col + d_col}, device_id_type=MESH)
 
     def start_sends(slot):
-        for route in routes(slot):
-            @pl.when(route[0])
-            def _():
-                copy_of(route, slot).start()
+        for condition, copy in copies(slot):
+            guarded(condition, copy.start)
 
     def wait_sends(slot):
-        for route in routes(slot):
-            @pl.when(route[0])
-            def _():
-                copy_of(route, slot).wait_send()
+        for condition, copy in copies(slot):
+            guarded(condition, copy.wait_send)
 
     def wait_recvs(slot):
-        came = [has[DOWN], has[UP], has[RIGHT], has[LEFT], has[DOWN] & has[RIGHT], has[DOWN] & has[LEFT],
-                has[UP] & has[RIGHT], has[UP] & has[LEFT]]
-        for route, condition in zip(routes(slot), came):
-            @pl.when(condition)
-            def _():
-                copy_of(route, slot).wait_recv()
+        for came, (_, copy) in zip((below, above, None, below, above), copies(slot)):
+            guarded(came, copy.wait_recv)
 
     def frame_copy(t, slot):
         return pltpu.make_async_copy(frames.at[jnp.minimum(t, steps - 1)], fr.at[slot], fr_sem.at[slot])
@@ -145,7 +136,7 @@
             edges[part][own, PAD:PAD + th, :] = value
             x[part][col_at(inner, 0, th - 8), :] = value[:th - 8]
             x[part][pl.ds(base(th - 1) + inner, 1), :] = value[th - 1:]
-            send[2, :, 128 * part:128 * (part + 1)] = value.astype(BF16)
+            send[SIDE, :, 128 * part:128 * (part + 1)] = value.astype(BF16)
         fill_row_sends()
 
     def fill_row_sends():
@@ -181,9 +172,10 @@
             lanes = slice(128 * part, 128 * (part + 1))
             for place, i in ((UP, -1), (DOWN, th)):
                 x[part][row_at(i), :] = land[slot, place, :, lanes].astype(F32)
-            for place, i, j, r in ((UL, -1, -1, 15), (UR, -1, tw, 0), (DL, th, -1, 15), (DR, th, tw, 0)):
-                x[part][pl.ds(base(i) + j, 1), :] = corner[slot, place, :, lanes].astype(F32)[r:r + 1, :]
-            e[beyond, PAD:PAD + th, :] = land[slot, RIGHT - col, :, lanes].astype(F32)
+                value = corner[slot, place, :, lanes].astype(F32)
+                value = jnp.where(col == 0, value[0:1, :], value[half - 1:, :])
+                x[part][pl.ds(base(i) + inner + 1 - 2 * col, 1), :] = value
+            e[beyond, PAD:PAD + th, :] = land[slot, SIDE, :, lanes].astype(F32)
             for k in range(3):
                 for i in (-1, th):
                     e[k, PAD + i:PAD + i + 1, :] = x[part][pl.ds(base(i) + inner - 1 + k, 1), :]
@@ -216,43 +208,41 @@
     frame_copy(1, 1).start()
     land[...] = jnp.zeros_like(land)
     corner[...] = jnp.zeros_like(corner)
+    barrier = pltpu.get_barrier_semaphore()
+    neighbours = 1 + 2 * above.astype(jnp.int32) + 2 * below.astype(jnp.int32)
+    for condition, d_row, d_col, *_ in routes(0):
+        guarded(condition, functools.partial(
+            pl.semaphore_signal, barrier, inc=1, device_id={"rows": row + d_row, "cols": col + d_col}, device_id_type=MESH))
     for ref in (em, et, xm, xt):
         ref[...] = jnp.zeros_like(ref)
     fx[...] = jnp.zeros_like(fx)
 
-    barrier = pltpu.get_barrier_semaphore()
-    neighbours = 0
-    for condition, d_row, d_col, *_ in routes(0):
-        neighbours = neighbours + condition.astype(jnp.int32)
-
-        @pl.when(condition)
-        def _():
-            pl.semaphore_signal(barrier, inc=1, device_id={"rows": row + d_row, "cols": col + d_col}, device_id_type=MESH)
-    pl.semaphore_wait(barrier, neighbours)
-
     frame_copy(0, 0).wait()
     for copy in state_copies:
         copy.wait()
 
-    @pl.loop(0, th)
-    def _(i):
-        at = pl.ds(pl.multiple_of(i * tw, tw), tw)
-        to = pl.ds(pl.multiple_of(base(0) + i * PITCH, 8), tw)
-        xm[to, :] = hb[at, 0:128].astype(F32)
-        tail = hb[at, 128:192].astype(F32)
-        xt[to, :] = jnp.concatenate([fr[0, at, :].astype(F32), tail], axis=1)
-        cm[at, :] = cb[at, 0:128]
-        tail = cb[at, 128:192]
-        ct[at, :] = jnp.concatenate([tail, tail], axis=1)
+    @pl.loop(0, th, step=8)
+    def _(first):
+        for k in range(8):
+            i = first + k
+            at = pl.ds(pl.multiple_of(i * tw, tw), tw)
+            to = pl.ds(pl.multiple_of(base(0) + i * PITCH, 8), tw)
+            xm[to, :] = hb[at, 0:128].astype(F32)
+            tail = hb[at, 128:192].astype(F32)
+            xt[to, :] = jnp.concatenate([fr[0, at, :].astype(F32), tail], axis=1)
+            cm[at, :] = cb[at, 0:128]
+            tail = cb[at, 128:192]
+            ct[at, :] = jnp.concatenate([tail, tail], axis=1)
 
     colm[...] = cm[pl.ds(inner, th, stride=tw), :]
     colt[...] = ct[pl.ds(inner, th, stride=tw), :]
     for part in range(2):
         value = x[part][col_at(inner), :]
         edges[part][own, PAD:PAD + th, :] = value
-        send[2, :, 128 * part:128 * (part + 1)] = value.astype(BF16)
+        send[SIDE, :, 128 * part:128 * (part + 1)] = value.astype(BF16)
     keep_beside()
     fill_row_sends()
+    pl.semaphore_wait(barrier, neighbours)
     start_sends(0)
     frame_copy(1, 1).wait()
     frame_copy(2, 0).start()
@@ -291,11 +281,19 @@
     cm[pl.ds(inner, th, stride=tw), :] = colm[...]
     ct[pl.ds(inner, th, stride=tw), :] = colt[...]
 
-    @pl.loop(0, th)
-    def _(i):
-        at = pl.ds(pl.multiple_of(i * tw, tw), tw)
+    for i in range(th):
+        at = pl.ds(i * tw, tw)
         c_out[at, 0:128] = cm[at, :]
         c_out[at, 128:192] = pltpu.roll(ct[at, :], 64, 1)[:, :64]
+
+
+def write_kernel(hs, c, hs_hbm, c_hbm, sems):
+    copies = [pltpu.make_async_copy(hs.at[t], hs_hbm.at[t], sems.at[t]) for t in range(hs.shape[0])]
+    copies.append(pltpu.make_async_copy(c, c_hbm, sems.at[hs.shape[0]]))
+    for copy in copies:
+        copy.start()
+    for copy in copies:
+        copy.wait()
 
 
 def lane_order(x, c):
@@ -333,11 +331,11 @@
                 pltpu.VMEM((cells, c_hid), BF16),
                 pltpu.VMEM((cells, c_hid), F32),
                 pltpu.VMEM((2, cells, c_in), BF16),
-                pltpu.VMEM((4, tw, 256), BF16),
-                pltpu.VMEM((2, 4, tw, 256), BF16),
-                pltpu.VMEM((2, 4, tw // 2, 256), BF16),
-                pltpu.SemaphoreType.DMA((8,)),
-                pltpu.SemaphoreType.DMA((2, 8)),
+                pltpu.VMEM((3, tw, 256), BF16),
+                pltpu.VMEM((2, 3, tw, 256), BF16),
+                pltpu.VMEM((2, 2, tw // 2, 256), BF16),
+                pltpu.SemaphoreType.DMA((5,)),
+                pltpu.SemaphoreType.DMA((2, 5)),
                 pltpu.SemaphoreType.DMA((2,)),
                 pltpu.SemaphoreType.DMA((5,)),
             ],
@@ -345,6 +343,14 @@
         )
         hidden, c_last = run(frames.reshape(steps, cells, c_in), w_in.reshape(9, c_in, -1), w_rec.reshape(9, c_hid, -1),
                              gate_bias, h_init.reshape(cells, c_hid), c_init.reshape(cells, c_hid))
+        hidden, c_last = pl.pallas_call(
+            write_kernel,
+            out_shape=(jax.ShapeDtypeStruct(hidden.shape, BF16), jax.ShapeDtypeStruct(c_last.shape, F32)),
+            in_specs=[vmem, vmem],
+            out_specs=(hbm, hbm),
+            scratch_shapes=[pltpu.SemaphoreType.DMA((steps + 1,))],
+            compiler_params=pltpu.CompilerParams(vmem_limit_bytes=1 << 20),
+        )(hidden, c_last)
         return hidden.reshape(steps, 1, th, tw, c_hid), c_last.reshape(1, th, tw, c_hid)
 
     return jax.shard_map(local_run, mesh=mesh, in_specs=(seq_spec, P(), P(), P(), state_spec, state_spec),

time: 155 us -> 150 us (0.968)
  local copies, waits for them, and re-layouts: 7.13 us -> 0 us
  Pallas kernels: 147 us -> 149 us
    unnamed x2 -> x0, local copies, waits for them, and re-layouts: 7.13 us -> none
    pallas_call x0 -> x1, Pallas kernels: none -> 6.42 us  [local_run(): pl.pallas_call(write_kernel, out_shape=(jax.ShapeDtypeStruct(hidden.shape...]
    pallas_call x1, Pallas kernels: 147 us -> 143 us  [local_run(): run(frames.reshape(steps, cells, c_in), w_in.reshape(9, c_in, -1), w_rec....]
where the time goes in v4:
time: 150 us
  Pallas kernels  149 us (99%)
    pallas_call x1, Pallas kernels, local_run(): run(frames.reshape(steps, cells, c_in), w_in.reshape(9, c_in, -1), w_rec....  143 us
    pallas_call x1, Pallas kernels, local_run(): pl.pallas_call(write_kernel, out_shape=(jax.ShapeDtypeStruct(hidden.shape...  6.42 us

profile of v4, /device:TPU:1, one launch (start us, length us, event | category | flops | bytes accessed | tf_op | source)
XLA Modules:
  0.0 149.6 jit_solution(6818754284307839120)
XLA Ops:
  0.6 142.5 %shard_map.77 = (bf16[32,1024,192]{2,1,0:T(8,128)(2,1)S(1)}, f32[1024,192]{1,0:T(8,128)S(1)}) custom-call(bf16[32,1024,64]{2,1,0:T(8,128)(2,1)} %bitcast.9, bf16[9,64,768]{2,1,0:T(8,128)(2,1)} %bitcast.12, bf16[9,192,768]{2,1,0:T(8,128)(2,1)} %bitcast.10, f32[768]{0:T(1024)} %gate_bias.1, bf16[1024,192]{1,0:T(8,128)(2,1)} %bitcast.13, f32[1024,192]{1,0:T(8,128)} %bitcast.11), custom_call_target="tpu_custom_call" | custom-call | tf_op jit(solution)/shard_map/pallas_call | solution.py:344
  143.2 6.4 %shard_map.78 = (bf16[32,1024,192]{2,1,0:T(8,128)(2,1)}, f32[1024,192]{1,0:T(8,128)}) custom-call(bf16[32,1024,192]{2,1,0:T(8,128)(2,1)S(1)} %get-tuple-element.6.hs, f32[1024,192]{1,0:T(8,128)S(1)} %get-tuple-element.7.c), custom_call_target="tpu_custom_call" | custom-call | tf_op jit(solution)/shard_map/pallas_call | solution.py:346

commit v5 on v4

--- a/solution.py
+++ b/solution.py
@@ -12,7 +12,7 @@
 PAD = 8
 PITCH = 40
 UP, DOWN, SIDE = range(3)
-BLOCK_A, BLOCK_B, BLOCK_C, BLOCK_D = (1, 8), (9, 9), (18, 8), (26, 4)
+BLOCK_A, BLOCK_B, BLOCK_C, BLOCK_D = (1, 10), (11, 10), (21, 5), (26, 4)
 RING_ROWS = (0, 30, 31)
 
 
@@ -64,12 +64,15 @@
     def frame_copy(t, slot):
         return pltpu.make_async_copy(frames.at[jnp.minimum(t, steps - 1)], fr.at[slot], fr_sem.at[slot])
 
-    weight_copies = [
-        pltpu.make_async_copy(w_rec.at[:, pl.ds(0, 128)], wraw.at[:, pl.ds(0, 128)], in_sem.at[0]),
-        pltpu.make_async_copy(w_in, wraw.at[:, pl.ds(128, 64)], in_sem.at[1]),
-        pltpu.make_async_copy(w_rec.at[:, pl.ds(128, 64)], wraw.at[:, pl.ds(192, 64)], in_sem.at[2]),
-    ]
-    state_copies = [pltpu.make_async_copy(h_hbm, hb, in_sem.at[3]), pltpu.make_async_copy(c_hbm, cb, in_sem.at[4])]
+    weight_copies = []
+    for k in range(3):
+        taps = pl.ds(3 * k, 3)
+        weight_copies.append([
+            pltpu.make_async_copy(w_rec.at[taps, pl.ds(0, 128)], wraw.at[taps, pl.ds(0, 128)], in_sem.at[2 + 3 * k]),
+            pltpu.make_async_copy(w_in.at[taps], wraw.at[taps, pl.ds(128, 64)], in_sem.at[3 + 3 * k]),
+            pltpu.make_async_copy(w_rec.at[taps, pl.ds(128, 64)], wraw.at[taps, pl.ds(192, 64)], in_sem.at[4 + 3 * k]),
+        ])
+    state_copies = [pltpu.make_async_copy(h_hbm, hb, in_sem.at[0]), pltpu.make_async_copy(c_hbm, cb, in_sem.at[1])]
 
     bias = lane_order(gate_bias[...].reshape(1, 768), 192)
     lane = lax.broadcasted_iota(jnp.int32, (tw, 128), 1)
@@ -149,8 +152,8 @@
             e[beside, PAD:PAD + th, :] = x[part][col_at(inner + 1 - beyond), :]
 
     def finish_step():
-        update_rows(gc, BLOCK_C, [25])
-        update_rows(gd, BLOCK_D, range(26, 30))
+        update_rows(gc, BLOCK_C, [sum(BLOCK_C) - 1])
+        update_rows(gd, BLOCK_D, range(BLOCK_D[0], sum(BLOCK_D)))
         update_row(gr, tw, 30)
         for part, e in enumerate(edges):
             x[part][col_at(inner, th - 8, 8), :] = e[own, PAD + th - 8:PAD + th, :]
@@ -183,8 +186,8 @@
     def late_blocks():
         ring_matmul()
         update_rows(ga, BLOCK_A, [1])
-        update_rows(gb, BLOCK_B, [17])
-        update_rows(gc, BLOCK_C, range(18, 25))
+        update_rows(gb, BLOCK_B, [sum(BLOCK_B) - 1])
+        update_rows(gc, BLOCK_C, range(BLOCK_C[0], sum(BLOCK_C) - 1))
         matmul(gd, BLOCK_D)
         update_ring()
 
@@ -195,15 +198,15 @@
             form_out(t)
         convert_frame(frame_slot)
         matmul(gb, BLOCK_B)
-        update_rows(ga, BLOCK_A, range(2, 8))
+        update_rows(ga, BLOCK_A, range(2, sum(BLOCK_A) - 1))
         matmul(gc, BLOCK_C)
-        update_rows(ga, BLOCK_A, [8])
-        update_rows(gb, BLOCK_B, range(9, 17))
-
-    for copy in state_copies:
+        update_rows(ga, BLOCK_A, [sum(BLOCK_A) - 1])
+        update_rows(gb, BLOCK_B, range(BLOCK_B[0], sum(BLOCK_B) - 1))
+
+    for copy in sum(weight_copies, []):
         copy.start()
     frame_copy(0, 0).start()
-    for copy in weight_copies:
+    for copy in state_copies:
         copy.start()
     frame_copy(1, 1).start()
     land[...] = jnp.zeros_like(land)
@@ -217,6 +220,15 @@
         ref[...] = jnp.zeros_like(ref)
     fx[...] = jnp.zeros_like(fx)
 
+    for k, chunk in enumerate(weight_copies):
+        for copy in chunk:
+            copy.wait()
+
+        @pl.loop(3 * k, 3 * k + 3)
+        def _(tap):
+            for first in range(0, 256, 64):
+                at = pl.ds(pl.multiple_of(tap * 256 + first, 64), 64)
+                ws[at, :] = lane_order(wraw[tap, first:first + 64, :], 192)
     frame_copy(0, 0).wait()
     for copy in state_copies:
         copy.wait()
@@ -246,14 +258,6 @@
     start_sends(0)
     frame_copy(1, 1).wait()
     frame_copy(2, 0).start()
-    for copy in weight_copies:
-        copy.wait()
-
-    @pl.loop(0, 9)
-    def _(tap):
-        for k in range(0, 256, 64):
-            at = pl.ds(pl.multiple_of(tap * 256 + k, 64), 64)
-            ws[at, :] = lane_order(wraw[tap, k:k + 64, :], 192)
     early_blocks(None, 1)
 
     def arrive(slot):
@@ -337,7 +341,7 @@
                 pltpu.SemaphoreType.DMA((5,)),
                 pltpu.SemaphoreType.DMA((2, 5)),
                 pltpu.SemaphoreType.DMA((2,)),
-                pltpu.SemaphoreType.DMA((5,)),
+                pltpu.SemaphoreType.DMA((11,)),
             ],
             compiler_params=pltpu.CompilerParams(collective_id=0, has_side_effects=True, vmem_limit_bytes=40 << 20),
         )

time: 150 us -> 149 us (level)
  no operation moved by 1% of the time
where the time goes in v5:
time: 149 us; the launch traced here: 148 us
  Pallas kernels  148 us (99%)
    pallas_call x1, Pallas kernels, local_run(): run(frames.reshape(steps, cells, c_in), w_in.reshape(9, c_in, -1), w_rec....  141 us
    pallas_call x1, Pallas kernels, local_run(): pl.pallas_call(write_kernel, out_shape=(jax.ShapeDtypeStruct(hidden.shape...  6.42 us

profile of v5, /device:TPU:1, one launch (start us, length us, event | category | flops | bytes accessed | tf_op | source)
XLA Modules:
  0.0 148.5 jit_solution(15208285165117622564)
XLA Ops:
  0.6 141.4 %shard_map.77 = (bf16[32,1024,192]{2,1,0:T(8,128)(2,1)S(1)}, f32[1024,192]{1,0:T(8,128)S(1)}) custom-call(bf16[32,1024,64]{2,1,0:T(8,128)(2,1)} %bitcast.9, bf16[9,64,768]{2,1,0:T(8,128)(2,1)} %bitcast.12, bf16[9,192,768]{2,1,0:T(8,128)(2,1)} %bitcast.10, f32[768]{0:T(1024)} %gate_bias.1, bf16[1024,192]{1,0:T(8,128)(2,1)} %bitcast.13, f32[1024,192]{1,0:T(8,128)} %bitcast.11), custom_call_target="tpu_custom_call" | custom-call | tf_op jit(solution)/shard_map/pallas_call | solution.py:348
  142.1 6.4 %shard_map.78 = (bf16[32,1024,192]{2,1,0:T(8,128)(2,1)}, f32[1024,192]{1,0:T(8,128)}) custom-call(bf16[32,1024,192]{2,1,0:T(8,128)(2,1)S(1)} %get-tuple-element.6.hs, f32[1024,192]{1,0:T(8,128)S(1)} %get-tuple-element.7.c), custom_call_target="tpu_custom_call" | custom-call | tf_op jit(solution)/shard_map/pallas_call | solution.py:350

commit v6 on v5

--- a/solution.py
+++ b/solution.py
@@ -294,8 +294,8 @@
 def write_kernel(hs, c, hs_hbm, c_hbm, sems):
     copies = [pltpu.make_async_copy(hs.at[t], hs_hbm.at[t], sems.at[t]) for t in range(hs.shape[0])]
     copies.append(pltpu.make_async_copy(c, c_hbm, sems.at[hs.shape[0]]))
-    for copy in copies:
-        copy.start()
+    for k, copy in enumerate(copies):
+        copy.start(priority=k % 2)
     for copy in copies:
         copy.wait()
 

time: 149 us -> 149 us (level)
  no operation moved by 1% of the time
where the time goes in v6:
time: 149 us; the launch traced here: 148 us
  Pallas kernels  148 us (99%)
    pallas_call x1, Pallas kernels, local_run(): run(frames.reshape(steps, cells, c_in), w_in.reshape(9, c_in, -1), w_rec....  141 us
    pallas_call x1, Pallas kernels, local_run(): pl.pallas_call(write_kernel, out_shape=(jax.ShapeDtypeStruct(hidden.shape...  6.4 us

profile of v6, /device:TPU:1, one launch (start us, length us, event | category | flops | bytes accessed | tf_op | source)
XLA Modules:
  0.0 148.5 jit_solution(10921408915603874524)
XLA Ops:
  0.6 141.4 %shard_map.77 = (bf16[32,1024,192]{2,1,0:T(8,128)(2,1)S(1)}, f32[1024,192]{1,0:T(8,128)S(1)}) custom-call(bf16[32,1024,64]{2,1,0:T(8,128)(2,1)} %bitcast.9, bf16[9,64,768]{2,1,0:T(8,128)(2,1)} %bitcast.12, bf16[9,192,768]{2,1,0:T(8,128)(2,1)} %bitcast.10, f32[768]{0:T(1024)} %gate_bias.1, bf16[1024,192]{1,0:T(8,128)(2,1)} %bitcast.13, f32[1024,192]{1,0:T(8,128)} %bitcast.11), custom_call_target="tpu_custom_call" | custom-call | tf_op jit(solution)/shard_map/pallas_call | solution.py:348
  142.1 6.4 %shard_map.78 = (bf16[32,1024,192]{2,1,0:T(8,128)(2,1)}, f32[1024,192]{1,0:T(8,128)}) custom-call(bf16[32,1024,192]{2,1,0:T(8,128)(2,1)S(1)} %get-tuple-element.6.hs, f32[1024,192]{1,0:T(8,128)S(1)} %get-tuple-element.7.c), custom_call_target="tpu_custom_call" | custom-call | tf_op jit(solution)/shard_map/pallas_call | solution.py:350
